TPU v7x, 128 devices: a whole 4x4x4 slice. The times are simulated.
128 devices in a mesh: gx: 4 (over y), gy: 4 (over z), gz: 8 (over x, core).
Axes of the slice: x: 4, y: 4, z: 4, core: 2. Of those that a mesh axis runs over, the one named last changes fastest.
Arguments:
- start: float32 [4, 4, 8, 1, 32, 1024], P('gx', 'gy', 'gz'), may hold values from -6 to 6
- stencils: float32 [6, 4, 4, 8, 32, 32], P(None, 'gx', 'gy', 'gz'), as said below
Outputs:
- basis: float32 [4, 4, 8, 1, 5, 32, 1024], P('gx', 'gy', 'gz')
- coefficients: float32 [1, 2, 5], replicated
Inputs may be any that keep to these rules, and one draw needn't show every extreme that they name: `stencils`: each of a patch's six matrices is symmetric positive definite.
All inputs are finite; a program needn't handle non-finite values.
Results may differ from a plain program's by a relative error of at most 0.0003.
Values sent between devices are 32-bit elements; how exact they have to be, the bound alone decides.
A program may use at most 128 MiB of HBM per device.

v0:
```python
import functools

import jax
import jax.numpy as jnp
from jax import lax
from jax.experimental import pallas as pl
from jax.experimental.pallas import tpu as pltpu
from jax.sharding import PartitionSpec as P

ITERS = 5
C = 32
MESH = pl.DeviceIdType.MESH
F32 = jnp.float32
AXES = ("gx", "gy", "gz")
DIRS = [
    (dx, dy, dz)
    for dx in (-1, 0, 1)
    for dy in (-1, 0, 1)
    for dz in (-1, 0, 1)
    if (dx, dy, dz) != (0, 0, 0)
]
SLOT = {d: i for i, d in enumerate(DIRS)}
SHRINK = 2.0**-17


def iota(shape, dim):
    return lax.broadcasted_iota(jnp.int32, shape, dim)


def roll(x, shift, axis):
    size = x.shape[axis]
    shift = shift % size
    return x if shift == 0 else pltpu.roll(x, shift, axis)


def swap(field):
    x = field.reshape(32, 8, 128)
    s, l = iota((1, 8, 128), 1), iota((1, 8, 128), 2)
    s1, l1 = (s // 2) % 2, l // 64
    r = roll(x, 64, 2)
    x = jnp.where(s1 == l1, x, jnp.where(s1 == 0, roll(r, -2, 1), roll(r, 2, 1)))
    s0, l0 = s % 2, (l // 32) % 2
    up, down = roll(roll(x, 32, 2), -1, 1), roll(roll(x, -32, 2), 1, 1)
    x = jnp.where(s0 == l0, x, jnp.where(s0 == 0, up, down))
    even = jnp.concatenate([x[t * 4 : t * 4 + 4] for t in range(0, 8, 2)], axis=0)
    odd = jnp.concatenate([x[t * 4 : t * 4 + 4] for t in range(1, 8, 2)], axis=0)
    half = s < 4
    top = jnp.where(half, even, roll(odd, 4, 1))
    bottom = jnp.where(half, roll(even, 4, 1), odd)
    parts = []
    for ai in range(4):
        for part in (top, bottom):
            for k in range(4):
                parts.append(part[k * 4 + ai : k * 4 + ai + 1])
    return jnp.concatenate(parts, axis=0).reshape(256, 128)


def wide(field):
    return jnp.concatenate([field[t * 32 : t * 32 + 32] for t in range(8)], axis=1)


def tall(field):
    return jnp.concatenate([field[:, t * 128 : t * 128 + 128] for t in range(8)], axis=0)


def dot(left, right):
    return lax.dot_general(
        left,
        right,
        (((1,), (0,)), ((), ())),
        precision=lax.Precision.HIGHEST,
        preferred_element_type=F32,
    )


def matvec(field, xmat_ref, ymat_ref, zmat_ref):
    first = dot(xmat_ref[...], wide(field))
    mass, stiff = swap(tall(first[:C])), swap(tall(first[C:]))
    second = dot(ymat_ref[...], jnp.concatenate([wide(stiff), wide(mass)], axis=0))
    third = jnp.concatenate([tall(second[:C]), tall(second[C:])], axis=1)
    return swap(dot(third, zmat_ref[...]))


def block_diagonal(matrix):
    zero = jnp.zeros((C, C), F32)
    rows = []
    for i in range(4):
        rows.append(jnp.concatenate([matrix if k == i else zero for k in range(4)], axis=1))
    return jnp.concatenate(rows, axis=0)


def weight_field(sizes, here):
    row, lane = iota((256, 128), 0), iota((256, 128), 1)
    places = (row % C, (row // C) * 4 + lane // C, lane % C)
    weight = jnp.ones((256, 128), F32)
    for place, size, at in zip(places, sizes, here):
        low = jnp.where(at > 0, 0.5, 1.0).astype(F32)
        high = jnp.where(at < size - 1, 0.5, 1.0).astype(F32)
        weight = weight * jnp.where(place == 0, low, jnp.where(place == C - 1, high, 1.0))
    return weight


def neighbour(sizes, here, step):
    fine = None
    for size, at, d in zip(sizes, here, step):
        if d != 0:
            inside = at > 0 if d < 0 else at < size - 1
            fine = inside if fine is None else jnp.logical_and(fine, inside)
    return fine, tuple(at + d for at, d in zip(here, step))


def pack(out_ref, send_ref):
    s, l = iota((8, 128), 0), iota((8, 128), 1)
    lower = lambda t, ai: out_ref[pl.ds(t * 32 + ai * 8, 8), :]
    zero = jnp.zeros((8, 128), F32)
    low, high = zero, zero
    for t in range(8):
        for ai in range(4):
            r = ai * 8 + t
            moved = roll(lower(t, ai), r, 1)
            low = jnp.where(l % C == r, moved, low)
            high = jnp.where(l % C == (r + C - 1) % C, moved, high)
    for dz, plane, base in ((-1, low, 0), (1, high, -31)):
        for dx in (-1, 0, 1):
            for dy in (-1, 0, 1):
                lanes = base - dx * 24 - dy * 103
                part = roll(roll(plane, lanes, 1), dx, 0)
                keep = None
                if dx != 0:
                    keep = (s == (7 if dx < 0 else 0)) & ((l % C) // 8 == (3 if dx < 0 else 0))
                if dy != 0:
                    mine = (l // C == (3 if dy < 0 else 0)) & (l % 8 == (7 if dy < 0 else 0))
                    keep = mine if keep is None else keep & mine
                send_ref[SLOT[(dx, dy, dz)]] = part if keep is None else jnp.where(keep, part, 0.0)
    for dx in (-1, 1):
        plane = out_ref[pl.ds(0 if dx < 0 else C - 1, 8, stride=C), :]
        send_ref[SLOT[(dx, 0, 0)]] = plane
        for dy in (-1, 1):
            part = roll(roll(plane, 96 if dy < 0 else 32, 1), dy, 0)
            keep = (s == (7 if dy < 0 else 0)) & (l // C == (3 if dy < 0 else 0))
            send_ref[SLOT[(dx, dy, 0)]] = jnp.where(keep, part, 0.0)
    for dy in (-1, 1):
        plane = zero
        for ai in range(4):
            piece = roll(lower(0 if dy < 0 else 7, ai), C * (ai + (0 if dy < 0 else 1)), 1)
            plane = jnp.where(l // C == ai, piece, plane)
        send_ref[SLOT[(0, dy, 0)]] = plane


def unpack(out_ref, got_ref):
    l = iota((8, 128), 1)
    near = (-1, 0, 1)
    for dx in (-1, 1):
        plane = sum(got_ref[SLOT[(dx, dy, 0)]] for dy in near)
        rows = pl.ds(C - 1 if dx < 0 else 0, 8, stride=C)
        out_ref[rows, :] = out_ref[rows, :] + plane
    low, high = (
        sum(got_ref[SLOT[(dx, dy, dz)]] for dx in near for dy in near) for dz in (1, -1)
    )
    first, last = got_ref[SLOT[(0, 1, 0)]], got_ref[SLOT[(0, -1, 0)]]
    for t in range(8):
        for ai in range(4):
            r = ai * 8 + t
            rows = pl.ds(t * 32 + ai * 8, 8)
            add = jnp.where(l % C == 0, roll(low, -r, 1), 0.0)
            add = add + jnp.where(l % C == C - 1, roll(high, 31 - r, 1), 0.0)
            if t == 0:
                add = add + jnp.where(l < C, roll(first, -C * ai, 1), 0.0)
            if t == 7:
                add = add + jnp.where(l >= 96, roll(last, 96 - C * ai, 1), 0.0)
            out_ref[rows, :] = out_ref[rows, :] + add


def kernel(
    sizes,
    start_ref,
    stencils_ref,
    basis_ref,
    coefficients_ref,
    out,
    vecs,
    images,
    weights,
    xmat,
    ymat,
    zmat,
    sends,
    gots,
    line,
    plane,
    coef,
    send_sem,
    got_sem,
    line_send,
    line_got,
    plane_send,
    plane_got,
):
    here = tuple(lax.axis_index(a) for a in AXES)
    nx, ny, nz = sizes
    gx, gy, gz = here
    line_peers = [(gx, gy, lax.rem(gz + k, nz)) for k in range(1, nz)]
    plane_peers = [
        (lax.rem(gx + k, nx), lax.rem(gy + m, ny), gz)
        for k in range(nx)
        for m in range(ny)
        if (k, m) != (0, 0)
    ]
    spans = [
        1 + jnp.where(at > 0, 1, 0) + jnp.where(at < size - 1, 1, 0)
        for at, size in zip(here, sizes)
    ]
    degree = spans[0] * spans[1] * spans[2] - 1
    degrees = sorted(
        {
            i * j * k - 1
            for i in span_set(nx)
            for j in span_set(ny)
            for k in span_set(nz)
        }
    )

    gots[...] = jnp.zeros_like(gots)

    barrier = pltpu.get_barrier_semaphore()
    for d in DIRS:
        fine, there = neighbour(sizes, here, d)

        @pl.when(fine)
        def _():
            pl.semaphore_signal(barrier, inc=1, device_id=there, device_id_type=MESH)

    for there in line_peers + plane_peers:
        pl.semaphore_signal(barrier, inc=1, device_id=there, device_id_type=MESH)

    vecs[...] = jnp.zeros_like(vecs)
    images[...] = jnp.zeros_like(images)
    coef[...] = jnp.zeros_like(coef)
    weights[...] = weight_field(sizes, here)
    kx, ky, kz, mx, my, mz = (stencils_ref[i] for i in range(6))
    xmat[...] = jnp.concatenate([mx, kx], axis=0)
    top = jnp.concatenate([my, ky], axis=1)
    ymat[...] = jnp.concatenate([top, jnp.concatenate([jnp.zeros((C, C), F32), my], axis=1)], axis=0)
    zmat[...] = jnp.concatenate([block_diagonal(mz.T), block_diagonal(kz.T)], axis=0)

    def exchange_start(par):
        pack(out, sends.at[par])
        if True:
            for d in sorted(DIRS, key=lambda d: -sum(abs(i) for i in d)):
                fine, there = neighbour(sizes, here, d)

                @pl.when(fine)
                def _():
                    pltpu.make_async_remote_copy(
                        src_ref=sends.at[par, SLOT[d]],
                        dst_ref=gots.at[par, SLOT[d]],
                        send_sem=send_sem.at[par],
                        recv_sem=got_sem.at[par],
                        device_id=there,
                        device_id_type=MESH,
                    ).start()

    def exchange_end(par):
        for n in degrees:

            @pl.when(degree == n)
            def _():
                both = pltpu.make_async_remote_copy(
                    src_ref=sends.at[par, pl.ds(0, n)],
                    dst_ref=gots.at[par, pl.ds(0, n)],
                    send_sem=send_sem.at[par],
                    recv_sem=got_sem.at[par],
                    device_id=line_peers[0],
                    device_id_type=MESH,
                )
                both.wait_recv()
                both.wait_send()

        unpack(out, gots.at[par])

    def reduce_start(buffer, at, peers, par, s_sem, g_sem, tile):
        buffer[par, at] = tile
        for there in peers:
            pltpu.make_async_remote_copy(
                src_ref=buffer.at[par, at],
                dst_ref=buffer.at[par, at],
                send_sem=s_sem.at[par],
                recv_sem=g_sem.at[par],
                device_id=there,
                device_id_type=MESH,
            ).start()

    def reduce_end(buffer, peers, par, s_sem, g_sem):
        both = pltpu.make_async_remote_copy(
            src_ref=buffer.at[par, pl.ds(0, len(peers))],
            dst_ref=buffer.at[par, pl.ds(0, len(peers))],
            send_sem=s_sem.at[par],
            recv_sem=g_sem.at[par],
            device_id=peers[0],
            device_id_type=MESH,
        )
        both.wait_recv()
        both.wait_send()
        return sum(buffer[par, k] for k in range(len(peers) + 1))

    def products(image):
        weighted = weights[...] * image
        pairs = [(vecs[i], weighted) for i in range(ITERS)]
        pairs += [(image, weighted), (vecs[0], weights[...] * vecs[0])]
        tile = jnp.zeros((8, 128), F32)
        for k, (left, right) in enumerate(pairs):
            lanes = jnp.sum(jnp.sum((left * right).reshape(32, 8, 128), axis=0), axis=0, keepdims=True)
            tile = jnp.where(iota((8, 128), 0) == k, lanes, tile)
        return tile

    def products_start(par, image):
        reduce_start(line, gz, line_peers, par, line_send, line_got, products(image))

    def products_middle(par):
        tile = reduce_end(line, line_peers, par, line_send, line_got)
        reduce_start(plane, gx * ny + gy, plane_peers, par, plane_send, plane_got, tile)

    def products_end(par):
        tile = reduce_end(plane, plane_peers, par, plane_send, plane_got)
        return jnp.sum(tile, axis=1, keepdims=True)

    def advance(j, totals, following):
        first = j == 0
        inverse = jnp.where(first, lax.rsqrt(totals[6:7]), 1.0)
        square = jnp.where(first, 1.0 / totals[6:7], 1.0)

        @pl.when(first)
        def _():
            vecs[0] = vecs[0] * inverse
            images[0] = images[0] * inverse

        heights = [totals[i : i + 1] * square for i in range(ITERS)]
        length = totals[5:6] * square
        beta = jnp.sqrt(length - sum(h * h for h in heights))
        alpha = sum(jnp.where(j == i, heights[i], 0.0) for i in range(ITERS))
        over = 1.0 / beta
        new = images[j]
        for i in range(ITERS):
            new = new - heights[i] * vecs[i]
        vecs[j + 1] = new * over
        s, l = iota((8, 128), 0), iota((8, 128), 1)
        entry = jnp.where(s == 0, alpha, jnp.where(s == 1, beta, 0.0))
        coef[...] = coef[...] + jnp.where(l == j, entry, 0.0)
        if following:
            image = out[...] * inverse
            for i in range(ITERS):
                image = image - heights[i] * images[i]
            images[j + 1] = image * over

    out[...] = tall(start_ref[...]) * weights[...] * SHRINK
    pl.semaphore_wait(barrier, degree + len(line_peers) + len(plane_peers))
    exchange_start(0)
    exchange_end(0)
    vecs[0] = out[...]
    out[...] = matvec(out[...], xmat, ymat, zmat)
    exchange_start(1)
    exchange_end(1)
    images[0] = out[...]

    def body(j, carry):
        par = lax.rem(j, 2)
        image = images[j]
        products_start(par, image)
        out[...] = matvec(image, xmat, ymat, zmat)
        exchange_start(par)
        products_middle(par)
        exchange_end(par)
        advance(j, products_end(par), True)
        return carry

    lax.fori_loop(0, ITERS - 1, body, 0)
    par = (ITERS - 1) % 2
    products_start(par, images[ITERS - 1])
    products_middle(par)
    advance(ITERS - 1, products_end(par), False)
    for i in range(ITERS):
        basis_ref[i] = wide(vecs[i + 1])
    coefficients_ref[...] = coef[0:2, 0:ITERS]


def span_set(size):
    return {1} if size == 1 else {2} if size == 2 else {2, 3}


def shards(sizes, start, stencils):
    nx, ny, nz = sizes
    vmem = pl.BlockSpec(memory_space=pltpu.VMEM)
    basis, coefficients = pl.pallas_call(
        functools.partial(kernel, sizes),
        out_shape=(
            jax.ShapeDtypeStruct((ITERS, C, C * C), F32),
            jax.ShapeDtypeStruct((2, ITERS), F32),
        ),
        in_specs=[vmem, vmem],
        out_specs=(vmem, vmem),
        scratch_shapes=[
            pltpu.VMEM((256, 128), F32),
            pltpu.VMEM((ITERS + 1, 256, 128), F32),
            pltpu.VMEM((ITERS, 256, 128), F32),
            pltpu.VMEM((256, 128), F32),
            pltpu.VMEM((2 * C, C), F32),
            pltpu.VMEM((2 * C, 2 * C), F32),
            pltpu.VMEM((256, 128), F32),
            pltpu.VMEM((2, len(DIRS), 8, 128), F32),
            pltpu.VMEM((2, len(DIRS), 8, 128), F32),
            pltpu.VMEM((2, nz, 8, 128), F32),
            pltpu.VMEM((2, nx * ny, 8, 128), F32),
            pltpu.VMEM((8, 128), F32),
        ]
        + [pltpu.SemaphoreType.DMA((2,))] * 6,
        compiler_params=pltpu.CompilerParams(collective_id=0, has_side_effects=True),
    )(start.reshape(C, C * C), stencils.reshape(6, C, C))
    return (
        basis.reshape(1, 1, 1, 1, ITERS, C, C * C),
        coefficients.reshape(1, 2, ITERS),
    )


def solution(mesh):
    sizes = tuple(mesh.shape[a] for a in AXES)
    return jax.shard_map(
        functools.partial(shards, sizes),
        mesh=mesh,
        in_specs=(P("gx", "gy", "gz", None, None, None), P(None, "gx", "gy", "gz", None, None)),
        out_specs=(P("gx", "gy", "gz", None, None, None, None), P()),
        check_vma=False,
    )
```

profile of v0, /device:TPU:1, one launch (start us, length us, event | category | flops | bytes accessed | tf_op | source)
XLA Modules:
  0.0 66.0 jit_solution(1408982253399670566)
XLA Ops:
  0.6 62.8 %shard_map.41 = (f32[5,32,1024]{2,1,0:T(8,128)}, f32[2,5]{1,0:T(2,128)}) custom-call(f32[32,1024]{1,0:T(8,128)} %bitcast.5, f32[6,32,32]{2,1,0:T(8,128)} %bitcast.6), custom_call_target="tpu_custom_call" | custom-call | tf_op jit(solution)/shard_map/pallas_call | solution.py:393
  63.5 0.0 copy-start
  63.5 2.0 %copy.6 = f32[1,1,1,1,5,32,1024]{6,5,4,3,2,1,0:T(8,128)} copy(f32[1,1,1,1,5,32,1024]{6,5,4,3,2,1,0:T(8,128)} %bitcast.4) | data formatting | bytes 1310720
  65.5 0.0 copy-done
  65.5 0.6 copy.7
Async XLA Ops:
  63.5 2.0 %copy-start = (f32[2,5]{1,0:T(2,128)S(1)}, f32[2,5]{1,0:T(2,128)}, u32[]{:S(2)}) copy-start(f32[2,5]{1,0:T(2,128)} %get-tuple-element.5) | copy-start | bytes 124
where the time goes:
time: 66.2 us; the launch traced here: 66 us
  Pallas kernels  62.8 us (95%)
  local copies, waits for them, and re-layouts  2.55 us (4%)
    pallas_call x1, Pallas kernels, shards(): pl.pallas_call(functools.partial(kernel, sizes), out_shape=(jax.ShapeDtyp...  62.8 us
    unnamed x4, local copies, waits for them, and re-layouts  2.55 us

commit v1 on v0

--- a/solution.py
+++ b/solution.py
@@ -186,26 +186,24 @@
     zmat,
     sends,
     gots,
-    line,
-    plane,
+    terms,
     coef,
     send_sem,
     got_sem,
-    line_send,
-    line_got,
-    plane_send,
-    plane_got,
+    term_send,
+    term_got,
 ):
     here = tuple(lax.axis_index(a) for a in AXES)
     nx, ny, nz = sizes
     gx, gy, gz = here
-    line_peers = [(gx, gy, lax.rem(gz + k, nz)) for k in range(1, nz)]
-    plane_peers = [
-        (lax.rem(gx + k, nx), lax.rem(gy + m, ny), gz)
-        for k in range(nx)
-        for m in range(ny)
-        if (k, m) != (0, 0)
-    ]
+    me = (gx * ny + gy) * nz + gz
+    hops = lambda k, size: min(k, size - k)
+    steps = sorted(
+        ((i, j, k) for i in range(nx) for j in range(ny) for k in range(nz)),
+        key=lambda d: -(hops(d[0], nx) + hops(d[1], ny) + hops(d[2], nz) / 2),
+    )
+    along = [[lax.rem(at + k, size) for k in range(size)] for at, size in zip(here, sizes)]
+    everyone = [tuple(along[a][d[a]] for a in range(3)) for d in steps if any(d)]
     spans = [
         1 + jnp.where(at > 0, 1, 0) + jnp.where(at < size - 1, 1, 0)
         for at, size in zip(here, sizes)
@@ -230,7 +228,7 @@
         def _():
             pl.semaphore_signal(barrier, inc=1, device_id=there, device_id_type=MESH)
 
-    for there in line_peers + plane_peers:
+    for there in everyone:
         pl.semaphore_signal(barrier, inc=1, device_id=there, device_id_type=MESH)
 
     vecs[...] = jnp.zeros_like(vecs)
@@ -270,7 +268,7 @@
                     dst_ref=gots.at[par, pl.ds(0, n)],
                     send_sem=send_sem.at[par],
                     recv_sem=got_sem.at[par],
-                    device_id=line_peers[0],
+                    device_id=everyone[0],
                     device_id_type=MESH,
                 )
                 both.wait_recv()
@@ -278,51 +276,46 @@
 
         unpack(out, gots.at[par])
 
-    def reduce_start(buffer, at, peers, par, s_sem, g_sem, tile):
-        buffer[par, at] = tile
-        for there in peers:
+    def products(image):
+        weighted = weights[...] * image
+        pairs = [(vecs[i], weighted) for i in range(ITERS)]
+        pairs += [(image, weighted), (vecs[0], weights[...] * vecs[0])]
+        s, l = iota((8, 128), 0), iota((8, 128), 1)
+        tile = jnp.zeros((8, 128), F32)
+        for k, (left, right) in enumerate(pairs):
+            lanes = jnp.sum(jnp.sum((left * right).reshape(32, 8, 128), axis=0), axis=0, keepdims=True)
+            tile = jnp.where(s == k, lanes, tile)
+        column = jnp.sum(tile, axis=1, keepdims=True)
+        return jnp.sum(jnp.where(s == l, column, 0.0), axis=0, keepdims=True)
+
+    def products_start(par, image):
+        mine = pl.ds(me, 1)
+        terms[par, mine] = products(image)
+        for there in everyone:
             pltpu.make_async_remote_copy(
-                src_ref=buffer.at[par, at],
-                dst_ref=buffer.at[par, at],
-                send_sem=s_sem.at[par],
-                recv_sem=g_sem.at[par],
+                src_ref=terms.at[par, mine],
+                dst_ref=terms.at[par, mine],
+                send_sem=term_send.at[par],
+                recv_sem=term_got.at[par],
                 device_id=there,
                 device_id_type=MESH,
             ).start()
 
-    def reduce_end(buffer, peers, par, s_sem, g_sem):
+    def products_end(par):
+        others = pl.ds(0, len(everyone))
         both = pltpu.make_async_remote_copy(
-            src_ref=buffer.at[par, pl.ds(0, len(peers))],
-            dst_ref=buffer.at[par, pl.ds(0, len(peers))],
-            send_sem=s_sem.at[par],
-            recv_sem=g_sem.at[par],
-            device_id=peers[0],
+            src_ref=terms.at[par, others],
+            dst_ref=terms.at[par, others],
+            send_sem=term_send.at[par],
+            recv_sem=term_got.at[par],
+            device_id=everyone[0],
             device_id_type=MESH,
         )
         both.wait_recv()
         both.wait_send()
-        return sum(buffer[par, k] for k in range(len(peers) + 1))
-
-    def products(image):
-        weighted = weights[...] * image
-        pairs = [(vecs[i], weighted) for i in range(ITERS)]
-        pairs += [(image, weighted), (vecs[0], weights[...] * vecs[0])]
-        tile = jnp.zeros((8, 128), F32)
-        for k, (left, right) in enumerate(pairs):
-            lanes = jnp.sum(jnp.sum((left * right).reshape(32, 8, 128), axis=0), axis=0, keepdims=True)
-            tile = jnp.where(iota((8, 128), 0) == k, lanes, tile)
-        return tile
-
-    def products_start(par, image):
-        reduce_start(line, gz, line_peers, par, line_send, line_got, products(image))
-
-    def products_middle(par):
-        tile = reduce_end(line, line_peers, par, line_send, line_got)
-        reduce_start(plane, gx * ny + gy, plane_peers, par, plane_send, plane_got, tile)
-
-    def products_end(par):
-        tile = reduce_end(plane, plane_peers, par, plane_send, plane_got)
-        return jnp.sum(tile, axis=1, keepdims=True)
+        row = jnp.sum(terms[par], axis=0, keepdims=True)
+        s, l = iota((8, 128), 0), iota((8, 128), 1)
+        return jnp.sum(jnp.where(s == l, row, 0.0), axis=1, keepdims=True)
 
     def advance(j, totals, following):
         first = j == 0
@@ -353,7 +346,7 @@
             images[j + 1] = image * over
 
     out[...] = tall(start_ref[...]) * weights[...] * SHRINK
-    pl.semaphore_wait(barrier, degree + len(line_peers) + len(plane_peers))
+    pl.semaphore_wait(barrier, degree + len(everyone))
     exchange_start(0)
     exchange_end(0)
     vecs[0] = out[...]
@@ -368,7 +361,6 @@
         products_start(par, image)
         out[...] = matvec(image, xmat, ymat, zmat)
         exchange_start(par)
-        products_middle(par)
         exchange_end(par)
         advance(j, products_end(par), True)
         return carry
@@ -376,7 +368,6 @@
     lax.fori_loop(0, ITERS - 1, body, 0)
     par = (ITERS - 1) % 2
     products_start(par, images[ITERS - 1])
-    products_middle(par)
     advance(ITERS - 1, products_end(par), False)
     for i in range(ITERS):
         basis_ref[i] = wide(vecs[i + 1])
@@ -408,11 +399,10 @@
             pltpu.VMEM((256, 128), F32),
             pltpu.VMEM((2, len(DIRS), 8, 128), F32),
             pltpu.VMEM((2, len(DIRS), 8, 128), F32),
-            pltpu.VMEM((2, nz, 8, 128), F32),
-            pltpu.VMEM((2, nx * ny, 8, 128), F32),
+            pltpu.VMEM((2, nx * ny * nz, 128), F32),
             pltpu.VMEM((8, 128), F32),
         ]
-        + [pltpu.SemaphoreType.DMA((2,))] * 6,
+        + [pltpu.SemaphoreType.DMA((2,))] * 4,
         compiler_params=pltpu.CompilerParams(collective_id=0, has_side_effects=True),
     )(start.reshape(C, C * C), stencils.reshape(6, C, C))
     return (

time: 66.2 us -> 56.2 us (0.85)
  Pallas kernels: 62.8 us -> 52.9 us
    pallas_call x1, Pallas kernels: 62.8 us -> 52.9 us  [shards(): pl.pallas_call(functools.partial(kernel, sizes), out_shape=(jax.ShapeDtyp...]
where the time goes in v1:
time: 56.2 us; the launch traced here: 56 us
  Pallas kernels  52.9 us (94%)
  local copies, waits for them, and re-layouts  2.55 us (5%)
  between operations  0.65 us (1%)
    pallas_call x1, Pallas kernels, shards(): pl.pallas_call(functools.partial(kernel, sizes), out_shape=(jax.ShapeDtyp...  52.9 us
    unnamed x4, local copies, waits for them, and re-layouts  2.55 us

profile of v1, /device:TPU:1, one launch (start us, length us, event | category | flops | bytes accessed | tf_op | source)
XLA Modules:
  0.0 56.0 jit_solution(16850221185578634350)
XLA Ops:
  0.6 52.9 %shard_map.41 = (f32[5,32,1024]{2,1,0:T(8,128)}, f32[2,5]{1,0:T(2,128)}) custom-call(f32[32,1024]{1,0:T(8,128)} %bitcast.5, f32[6,32,32]{2,1,0:T(8,128)} %bitcast.6), custom_call_target="tpu_custom_call" | custom-call | tf_op jit(solution)/shard_map/pallas_call | solution.py:384
  53.5 0.0 copy-start
  53.5 2.0 %copy.6 = f32[1,1,1,1,5,32,1024]{6,5,4,3,2,1,0:T(8,128)} copy(f32[1,1,1,1,5,32,1024]{6,5,4,3,2,1,0:T(8,128)} %bitcast.4) | data formatting | bytes 1310720
  55.5 0.0 copy-done
  55.5 0.6 %copy.7 = f32[1,2,5]{2,1,0:T(2,128)} copy(f32[1,2,5]{2,1,0:T(2,128)S(1)} %bitcast.7) | data formatting | bytes 80
Async XLA Ops:
  53.5 2.0 %copy-start = (f32[2,5]{1,0:T(2,128)S(1)}, f32[2,5]{1,0:T(2,128)}, u32[]{:S(2)}) copy-start(f32[2,5]{1,0:T(2,128)} %get-tuple-element.5) | copy-start | bytes 124

commit v2 on v1

--- a/solution.py
+++ b/solution.py
@@ -107,6 +107,37 @@
             inside = at > 0 if d < 0 else at < size - 1
             fine = inside if fine is None else jnp.logical_and(fine, inside)
     return fine, tuple(at + d for at, d in zip(here, step))
+
+
+def axis_leaps(size, at, step):
+    if size <= step + 1:
+        return []
+    if size == 2 * step:
+        return [(True, lax.rem(at + step, size))]
+    return [(at >= step, at - step), (at < size - step, at + step)]
+
+
+def leaps(sizes, here, step):
+    choices = [[(True, at)] + axis_leaps(size, at, step) for size, at in zip(sizes, here)]
+    found = []
+    for i, x in enumerate(choices[0]):
+        for j, y in enumerate(choices[1]):
+            for k, z in enumerate(choices[2]):
+                if i + j + k > 0:
+                    tests = [c[0] for c in (x, y, z) if c[0] is not True]
+                    fine = functools.reduce(jnp.logical_and, tests) if tests else True
+                    found.append((fine, (x[1], y[1], z[1])))
+    return found
+
+
+def leap_count(sizes, here, step):
+    total = 1
+    for size, at in zip(sizes, here):
+        count = 1
+        for fine, _ in axis_leaps(size, at, step):
+            count = count + (1 if fine is True else jnp.where(fine, 1, 0))
+        total = total * count
+    return total - 1
 
 
 def pack(out_ref, send_ref):
@@ -173,10 +204,14 @@
 
 def kernel(
     sizes,
+    start_hbm,
+    stencils_hbm,
+    basis_ref,
+    coefficients_ref,
     start_ref,
     stencils_ref,
-    basis_ref,
-    coefficients_ref,
+    wides,
+    small,
     out,
     vecs,
     images,
@@ -192,6 +227,10 @@
     got_sem,
     term_send,
     term_got,
+    in_sem,
+    out_sem,
+    near,
+    far,
 ):
     here = tuple(lax.axis_index(a) for a in AXES)
     nx, ny, nz = sizes
@@ -218,8 +257,13 @@
         }
     )
 
+    inputs = [
+        pltpu.make_async_copy(start_hbm, start_ref, in_sem.at[0]),
+        pltpu.make_async_copy(stencils_hbm, stencils_ref, in_sem.at[1]),
+    ]
+    for copy in inputs:
+        copy.start()
     gots[...] = jnp.zeros_like(gots)
-
     barrier = pltpu.get_barrier_semaphore()
     for d in DIRS:
         fine, there = neighbour(sizes, here, d)
@@ -227,19 +271,27 @@
         @pl.when(fine)
         def _():
             pl.semaphore_signal(barrier, inc=1, device_id=there, device_id_type=MESH)
-
-    for there in everyone:
-        pl.semaphore_signal(barrier, inc=1, device_id=there, device_id_type=MESH)
 
     vecs[...] = jnp.zeros_like(vecs)
     images[...] = jnp.zeros_like(images)
     coef[...] = jnp.zeros_like(coef)
     weights[...] = weight_field(sizes, here)
+    for copy in inputs:
+        copy.wait()
     kx, ky, kz, mx, my, mz = (stencils_ref[i] for i in range(6))
     xmat[...] = jnp.concatenate([mx, kx], axis=0)
     top = jnp.concatenate([my, ky], axis=1)
     ymat[...] = jnp.concatenate([top, jnp.concatenate([jnp.zeros((C, C), F32), my], axis=1)], axis=0)
     zmat[...] = jnp.concatenate([block_diagonal(mz.T), block_diagonal(kz.T)], axis=0)
+
+    def greet(fine, there, semaphore):
+        def signal():
+            pl.semaphore_signal(semaphore, inc=1, device_id=there, device_id_type=MESH)
+
+        if fine is True:
+            signal()
+        else:
+            pl.when(fine)(signal)
 
     def exchange_start(par):
         pack(out, sends.at[par])
@@ -345,13 +397,26 @@
                 image = image - heights[i] * images[i]
             images[j + 1] = image * over
 
+    def leaving(i):
+        return pltpu.make_async_copy(wides.at[i - 1], basis_ref.at[i - 1], out_sem.at[i - 1])
+
+    def leave(i):
+        wides[i - 1] = wide(vecs[i])
+        return leaving(i)
+
     out[...] = tall(start_ref[...]) * weights[...] * SHRINK
-    pl.semaphore_wait(barrier, degree + len(everyone))
+    pl.semaphore_wait(barrier, degree)
     exchange_start(0)
     exchange_end(0)
+    for fine, there in leaps(sizes, here, 2):
+        greet(fine, there, near)
     vecs[0] = out[...]
     out[...] = matvec(out[...], xmat, ymat, zmat)
+    pl.semaphore_wait(near, leap_count(sizes, here, 2))
+    for fine, there in leaps(sizes, here, 4):
+        greet(fine, there, far)
     exchange_start(1)
+    pl.semaphore_wait(far, leap_count(sizes, here, 4))
     exchange_end(1)
     images[0] = out[...]
 
@@ -361,6 +426,11 @@
         products_start(par, image)
         out[...] = matvec(image, xmat, ymat, zmat)
         exchange_start(par)
+
+        @pl.when(j > 0)
+        def _():
+            leave(j).start()
+
         exchange_end(par)
         advance(j, products_end(par), True)
         return carry
@@ -368,10 +438,15 @@
     lax.fori_loop(0, ITERS - 1, body, 0)
     par = (ITERS - 1) % 2
     products_start(par, images[ITERS - 1])
+    leave(ITERS - 1).start()
     advance(ITERS - 1, products_end(par), False)
-    for i in range(ITERS):
-        basis_ref[i] = wide(vecs[i + 1])
-    coefficients_ref[...] = coef[0:2, 0:ITERS]
+    leave(ITERS).start()
+    small[...] = coef[0:2, 0:ITERS]
+    last = pltpu.make_async_copy(small, coefficients_ref, out_sem.at[ITERS])
+    last.start()
+    for i in range(1, ITERS + 1):
+        leaving(i).wait()
+    last.wait()
 
 
 def span_set(size):
@@ -380,16 +455,21 @@
 
 def shards(sizes, start, stencils):
     nx, ny, nz = sizes
-    vmem = pl.BlockSpec(memory_space=pltpu.VMEM)
+    hbm = pl.BlockSpec(memory_space=pltpu.HBM)
+    anyw = pl.BlockSpec(memory_space=pl.ANY)
     basis, coefficients = pl.pallas_call(
         functools.partial(kernel, sizes),
         out_shape=(
             jax.ShapeDtypeStruct((ITERS, C, C * C), F32),
             jax.ShapeDtypeStruct((2, ITERS), F32),
         ),
-        in_specs=[vmem, vmem],
-        out_specs=(vmem, vmem),
+        in_specs=[hbm, hbm],
+        out_specs=(anyw, anyw),
         scratch_shapes=[
+            pltpu.VMEM((C, C * C), F32),
+            pltpu.VMEM((6, C, C), F32),
+            pltpu.VMEM((ITERS, C, C * C), F32),
+            pltpu.VMEM((2, ITERS), F32),
             pltpu.VMEM((256, 128), F32),
             pltpu.VMEM((ITERS + 1, 256, 128), F32),
             pltpu.VMEM((ITERS, 256, 128), F32),
@@ -402,7 +482,8 @@
             pltpu.VMEM((2, nx * ny * nz, 128), F32),
             pltpu.VMEM((8, 128), F32),
         ]
-        + [pltpu.SemaphoreType.DMA((2,))] * 4,
+        + [pltpu.SemaphoreType.DMA((2,))] * 5
+        + [pltpu.SemaphoreType.DMA((ITERS + 1,)), pltpu.SemaphoreType.REGULAR, pltpu.SemaphoreType.REGULAR],
         compiler_params=pltpu.CompilerParams(collective_id=0, has_side_effects=True),
     )(start.reshape(C, C * C), stencils.reshape(6, C, C))
     return (

time: 56.2 us -> 55.4 us (0.986)
  Pallas kernels: 52.9 us -> 52 us
    pallas_call x1, Pallas kernels: 52.9 us -> 52 us  [shards(): pl.pallas_call(functools.partial(kernel, sizes), out_shape=(jax.ShapeDtyp...]
where the time goes in v2:
time: 55.4 us; the launch traced here: 55.2 us
  Pallas kernels  52 us (94%)
  local copies, waits for them, and re-layouts  2.55 us (5%)
  between operations  0.65 us (1%)
    pallas_call x1, Pallas kernels, shards(): pl.pallas_call(functools.partial(kernel, sizes), out_shape=(jax.ShapeDtyp...  52 us
    unnamed x4, local copies, waits for them, and re-layouts  2.55 us

profile of v2, /device:TPU:1, one launch (start us, length us, event | category | flops | bytes accessed | tf_op | source)
XLA Modules:
  0.0 55.2 jit_solution(15086982676425444381)
XLA Ops:
  0.6 52.0 %shard_map.41 = (f32[5,32,1024]{2,1,0:T(8,128)}, f32[2,5]{1,0:T(2,128)}) custom-call(f32[32,1024]{1,0:T(8,128)} %bitcast.5, f32[6,32,32]{2,1,0:T(8,128)} %bitcast.6), custom_call_target="tpu_custom_call" | custom-call | tf_op jit(solution)/shard_map/pallas_call | solution.py:460
  52.7 0.0 copy-start
  52.7 2.0 %copy.6 = f32[1,1,1,1,5,32,1024]{6,5,4,3,2,1,0:T(8,128)} copy(f32[1,1,1,1,5,32,1024]{6,5,4,3,2,1,0:T(8,128)} %bitcast.4) | data formatting | bytes 1310720
  54.7 0.0 copy-done
  54.7 0.6 %copy.7 = f32[1,2,5]{2,1,0:T(2,128)} copy(f32[1,2,5]{2,1,0:T(2,128)S(1)} %bitcast.7) | data formatting | bytes 80
Async XLA Ops:
  52.7 2.0 %copy-start = (f32[2,5]{1,0:T(2,128)S(1)}, f32[2,5]{1,0:T(2,128)}, u32[]{:S(2)}) copy-start(f32[2,5]{1,0:T(2,128)} %get-tuple-element.5) | copy-start | bytes 124

commit v3 on v1

--- a/solution.py
+++ b/solution.py
@@ -173,13 +173,17 @@
 
 def kernel(
     sizes,
+    start_hbm,
+    stencils_hbm,
+    basis_ref,
+    coefficients_ref,
     start_ref,
     stencils_ref,
-    basis_ref,
-    coefficients_ref,
+    wides,
+    small,
     out,
+    powers,
     vecs,
-    images,
     weights,
     xmat,
     ymat,
@@ -187,11 +191,12 @@
     sends,
     gots,
     terms,
-    coef,
     send_sem,
     got_sem,
     term_send,
     term_got,
+    in_sem,
+    out_sem,
 ):
     here = tuple(lax.axis_index(a) for a in AXES)
     nx, ny, nz = sizes
@@ -218,23 +223,20 @@
         }
     )
 
+    inputs = [
+        pltpu.make_async_copy(start_hbm, start_ref, in_sem.at[0]),
+        pltpu.make_async_copy(stencils_hbm, stencils_ref, in_sem.at[1]),
+    ]
+    for copy in inputs:
+        copy.start()
     gots[...] = jnp.zeros_like(gots)
-
     barrier = pltpu.get_barrier_semaphore()
-    for d in DIRS:
-        fine, there = neighbour(sizes, here, d)
-
-        @pl.when(fine)
-        def _():
-            pl.semaphore_signal(barrier, inc=1, device_id=there, device_id_type=MESH)
-
     for there in everyone:
         pl.semaphore_signal(barrier, inc=1, device_id=there, device_id_type=MESH)
 
-    vecs[...] = jnp.zeros_like(vecs)
-    images[...] = jnp.zeros_like(images)
-    coef[...] = jnp.zeros_like(coef)
     weights[...] = weight_field(sizes, here)
+    for copy in inputs:
+        copy.wait()
     kx, ky, kz, mx, my, mz = (stencils_ref[i] for i in range(6))
     xmat[...] = jnp.concatenate([mx, kx], axis=0)
     top = jnp.concatenate([my, ky], axis=1)
@@ -276,102 +278,146 @@
 
         unpack(out, gots.at[par])
 
-    def products(image):
-        weighted = weights[...] * image
-        pairs = [(vecs[i], weighted) for i in range(ITERS)]
-        pairs += [(image, weighted), (vecs[0], weights[...] * vecs[0])]
+    def gather_start(k, pairs):
         s, l = iota((8, 128), 0), iota((8, 128), 1)
         tile = jnp.zeros((8, 128), F32)
-        for k, (left, right) in enumerate(pairs):
+        for i, (left, right) in enumerate(pairs):
             lanes = jnp.sum(jnp.sum((left * right).reshape(32, 8, 128), axis=0), axis=0, keepdims=True)
-            tile = jnp.where(s == k, lanes, tile)
+            tile = jnp.where(s == i, lanes, tile)
         column = jnp.sum(tile, axis=1, keepdims=True)
-        return jnp.sum(jnp.where(s == l, column, 0.0), axis=0, keepdims=True)
-
-    def products_start(par, image):
+        gather_row(k, jnp.sum(jnp.where(s == l, column, 0.0), axis=0, keepdims=True))
+
+    def gather_row(k, row):
         mine = pl.ds(me, 1)
-        terms[par, mine] = products(image)
+        terms[k, mine] = row
         for there in everyone:
             pltpu.make_async_remote_copy(
-                src_ref=terms.at[par, mine],
-                dst_ref=terms.at[par, mine],
-                send_sem=term_send.at[par],
-                recv_sem=term_got.at[par],
+                src_ref=terms.at[k, mine],
+                dst_ref=terms.at[k, mine],
+                send_sem=term_send.at[k],
+                recv_sem=term_got.at[k],
                 device_id=there,
                 device_id_type=MESH,
             ).start()
 
-    def products_end(par):
+    def gather_end(k, count):
         others = pl.ds(0, len(everyone))
         both = pltpu.make_async_remote_copy(
-            src_ref=terms.at[par, others],
-            dst_ref=terms.at[par, others],
-            send_sem=term_send.at[par],
-            recv_sem=term_got.at[par],
+            src_ref=terms.at[k, others],
+            dst_ref=terms.at[k, others],
+            send_sem=term_send.at[k],
+            recv_sem=term_got.at[k],
             device_id=everyone[0],
             device_id_type=MESH,
         )
         both.wait_recv()
         both.wait_send()
-        row = jnp.sum(terms[par], axis=0, keepdims=True)
+        row = jnp.sum(terms[k], axis=0, keepdims=True)
         s, l = iota((8, 128), 0), iota((8, 128), 1)
-        return jnp.sum(jnp.where(s == l, row, 0.0), axis=1, keepdims=True)
-
-    def advance(j, totals, following):
-        first = j == 0
-        inverse = jnp.where(first, lax.rsqrt(totals[6:7]), 1.0)
-        square = jnp.where(first, 1.0 / totals[6:7], 1.0)
-
-        @pl.when(first)
-        def _():
-            vecs[0] = vecs[0] * inverse
-            images[0] = images[0] * inverse
-
-        heights = [totals[i : i + 1] * square for i in range(ITERS)]
-        length = totals[5:6] * square
-        beta = jnp.sqrt(length - sum(h * h for h in heights))
-        alpha = sum(jnp.where(j == i, heights[i], 0.0) for i in range(ITERS))
-        over = 1.0 / beta
-        new = images[j]
-        for i in range(ITERS):
-            new = new - heights[i] * vecs[i]
-        vecs[j + 1] = new * over
-        s, l = iota((8, 128), 0), iota((8, 128), 1)
-        entry = jnp.where(s == 0, alpha, jnp.where(s == 1, beta, 0.0))
-        coef[...] = coef[...] + jnp.where(l == j, entry, 0.0)
-        if following:
-            image = out[...] * inverse
-            for i in range(ITERS):
-                image = image - heights[i] * images[i]
-            images[j + 1] = image * over
+        column = jnp.sum(jnp.where(s == l, row, 0.0), axis=1, keepdims=True)
+        return [column[i : i + 1] for i in range(count)]
+
+    def leaving(i):
+        return pltpu.make_async_copy(wides.at[i - 1], basis_ref.at[i - 1], out_sem.at[i - 1])
+
+    def settle(i, image, height):
+        new = image
+        for k in range(i):
+            new = new - height[k] * vecs[k]
+        new = new * (1.0 / height[i])
+        if i < ITERS:
+            vecs[i] = new
+        if i > 0:
+            wides[i - 1] = wide(new)
+            leaving(i).start()
+
+    def heights(products, known):
+        *with_known, with_last, square = products
+        i = len(known)
+        found = list(with_known)
+        last = with_last
+        for k in range(i - 1):
+            last = last - known[i - 1][k] * found[k]
+        found.append(last / known[i - 1][i - 1])
+        for value in found:
+            square = square - value * value
+        found.append(jnp.sqrt(square))
+        return found
 
     out[...] = tall(start_ref[...]) * weights[...] * SHRINK
-    pl.semaphore_wait(barrier, degree + len(everyone))
+    pl.semaphore_wait(barrier, len(everyone))
     exchange_start(0)
+    trace = [jnp.sum(jnp.where(iota((C, C), 0) == iota((C, C), 1), m, 0.0), keepdims=True) / C for m in (kx, ky, kz, mx, my, mz)]
+    mean = trace[0] * trace[4] * trace[5] + trace[3] * trace[1] * trace[5] + trace[3] * trace[4] * trace[2]
+    gather_row(0, jnp.broadcast_to(mean / (nx * ny * nz), (1, 128)))
     exchange_end(0)
-    vecs[0] = out[...]
-    out[...] = matvec(out[...], xmat, ymat, zmat)
+    powers[0] = out[...]
+
+    out[...] = matvec(powers[0], xmat, ymat, zmat)
     exchange_start(1)
     exchange_end(1)
-    images[0] = out[...]
-
-    def body(j, carry):
-        par = lax.rem(j, 2)
-        image = images[j]
-        products_start(par, image)
-        out[...] = matvec(image, xmat, ymat, zmat)
-        exchange_start(par)
-        exchange_end(par)
-        advance(j, products_end(par), True)
-        return carry
-
-    lax.fori_loop(0, ITERS - 1, body, 0)
-    par = (ITERS - 1) % 2
-    products_start(par, images[ITERS - 1])
-    advance(ITERS - 1, products_end(par), False)
-    for i in range(ITERS):
-        basis_ref[i] = wide(vecs[i + 1])
-    coefficients_ref[...] = coef[0:2, 0:ITERS]
+    powers[1] = out[...]
+
+    out[...] = matvec(powers[1], xmat, ymat, zmat)
+    exchange_start(0)
+    weighted = weights[...] * powers[1]
+    gather_start(1, [(powers[0], weights[...] * powers[0]), (powers[0], weighted), (powers[1], weighted)])
+    (size,) = gather_end(0, 1)
+    exchange_end(0)
+    powers[2] = out[...] * (1.0 / size)
+
+    triangle, alphas, betas = [], [], []
+    for j in range(2, ITERS + 1):
+        if j < ITERS:
+            out[...] = matvec(powers[j], xmat, ymat, zmat)
+            exchange_start((j + 1) % 2)
+        weighted = weights[...] * powers[j]
+        earlier = [vecs[k] if j > 2 else powers[0] for k in range(j - 1)]
+        gather_start(j, [(v, weighted) for v in earlier + [powers[j - 1], powers[j]]])
+        rounds = [j - 1] if j < ITERS else [j - 1, j]
+        for k in rounds:
+            if k == 1:
+                square, *rest = gather_end(1, 3)
+                triangle.append([jnp.sqrt(square)])
+                settle(0, powers[0], triangle[0])
+                triangle.append(heights(rest, triangle))
+                hess = {(1, 0): 1.0, (1, 1): 0.0, (2, 1): size}
+            else:
+                products = gather_end(k, k + 1)
+                if k == 2:
+                    products[0] = products[0] / triangle[0][0]
+                triangle.append(heights(products, triangle))
+            settle(k, powers[k], triangle[k])
+            i = k - 1
+            diagonal = triangle[k][i] * hess[(k, i)] / triangle[i][i]
+            if i > 0:
+                diagonal = diagonal + hess[(i, i)] - triangle[i][i - 1] * hess[(i, i - 1)] / triangle[i - 1][i - 1]
+            alphas.append(diagonal)
+            betas.append(triangle[k][k] * hess[(k, i)] / triangle[i][i])
+        if j < ITERS:
+            exchange_end((j + 1) % 2)
+            new = out[...] - alphas[j - 2] * powers[j]
+            lead = betas[j - 2]
+            if j == 2:
+                lead = lead * triangle[0][0]
+            else:
+                behind = betas[j - 3]
+                if j == 3:
+                    behind = behind / triangle[0][0]
+                new = new - behind * powers[j - 1]
+            powers[j + 1] = new * (1.0 / lead)
+            hess[(j, j)], hess[(j + 1, j)] = alphas[j - 2], lead
+
+    s, l = iota((8, 128), 0), iota((8, 128), 1)
+    tile = jnp.zeros((8, 128), F32)
+    for j in range(ITERS):
+        tile = jnp.where((s == 0) & (l == j), alphas[j], jnp.where((s == 1) & (l == j), betas[j], tile))
+    small[...] = tile[0:2, 0:ITERS]
+    last = pltpu.make_async_copy(small, coefficients_ref, out_sem.at[ITERS])
+    last.start()
+    for i in range(1, ITERS + 1):
+        leaving(i).wait()
+    last.wait()
 
 
 def span_set(size):
@@ -380,16 +426,21 @@
 
 def shards(sizes, start, stencils):
     nx, ny, nz = sizes
-    vmem = pl.BlockSpec(memory_space=pltpu.VMEM)
+    hbm = pl.BlockSpec(memory_space=pltpu.HBM)
+    anyw = pl.BlockSpec(memory_space=pl.ANY)
     basis, coefficients = pl.pallas_call(
         functools.partial(kernel, sizes),
         out_shape=(
             jax.ShapeDtypeStruct((ITERS, C, C * C), F32),
             jax.ShapeDtypeStruct((2, ITERS), F32),
         ),
-        in_specs=[vmem, vmem],
-        out_specs=(vmem, vmem),
+        in_specs=[hbm, hbm],
+        out_specs=(anyw, anyw),
         scratch_shapes=[
+            pltpu.VMEM((C, C * C), F32),
+            pltpu.VMEM((6, C, C), F32),
+            pltpu.VMEM((ITERS, C, C * C), F32),
+            pltpu.VMEM((2, ITERS), F32),
             pltpu.VMEM((256, 128), F32),
             pltpu.VMEM((ITERS + 1, 256, 128), F32),
             pltpu.VMEM((ITERS, 256, 128), F32),
@@ -399,10 +450,11 @@
             pltpu.VMEM((256, 128), F32),
             pltpu.VMEM((2, len(DIRS), 8, 128), F32),
             pltpu.VMEM((2, len(DIRS), 8, 128), F32),
-            pltpu.VMEM((2, nx * ny * nz, 128), F32),
-            pltpu.VMEM((8, 128), F32),
+            pltpu.VMEM((ITERS + 1, nx * ny * nz, 128), F32),
         ]
-        + [pltpu.SemaphoreType.DMA((2,))] * 4,
+        + [pltpu.SemaphoreType.DMA((2,))] * 2
+        + [pltpu.SemaphoreType.DMA((ITERS + 1,))] * 2
+        + [pltpu.SemaphoreType.DMA((2,)), pltpu.SemaphoreType.DMA((ITERS + 1,))],
         compiler_params=pltpu.CompilerParams(collective_id=0, has_side_effects=True),
     )(start.reshape(C, C * C), stencils.reshape(6, C, C))
     return (

time: 56.2 us -> 51.3 us (0.913)
  Pallas kernels: 52.9 us -> 48 us
    pallas_call x1, Pallas kernels: 52.9 us -> 48 us  [shards(): pl.pallas_call(functools.partial(kernel, sizes), out_shape=(jax.ShapeDtyp...]
where the time goes in v3:
time: 51.3 us; the launch traced here: 51.2 us
  Pallas kernels  48 us (94%)
  local copies, waits for them, and re-layouts  2.55 us (5%)
  between operations  0.65 us (1%)
    pallas_call x1, Pallas kernels, shards(): pl.pallas_call(functools.partial(kernel, sizes), out_shape=(jax.ShapeDtyp...  48 us
    unnamed x4, local copies, waits for them, and re-layouts  2.55 us

profile of v3, /device:TPU:1, one launch (start us, length us, event | category | flops | bytes accessed | tf_op | source)
XLA Modules:
  0.0 51.2 jit_solution(16119900774960599654)
XLA Ops:
  0.6 48.0 %shard_map.41 = (f32[5,32,1024]{2,1,0:T(8,128)}, f32[2,5]{1,0:T(2,128)}) custom-call(f32[32,1024]{1,0:T(8,128)} %bitcast.5, f32[6,32,32]{2,1,0:T(8,128)} %bitcast.6), custom_call_target="tpu_custom_call" | custom-call | tf_op jit(solution)/shard_map/pallas_call | solution.py:431
  48.6 0.0 copy-start
  48.6 2.0 %copy.6 = f32[1,1,1,1,5,32,1024]{6,5,4,3,2,1,0:T(8,128)} copy(f32[1,1,1,1,5,32,1024]{6,5,4,3,2,1,0:T(8,128)} %bitcast.4) | data formatting | bytes 1310720
  50.6 0.0 copy-done
  50.6 0.6 %copy.7 = f32[1,2,5]{2,1,0:T(2,128)} copy(f32[1,2,5]{2,1,0:T(2,128)S(1)} %bitcast.7) | data formatting | bytes 80
Async XLA Ops:
  48.6 2.0 %copy-start = (f32[2,5]{1,0:T(2,128)S(1)}, f32[2,5]{1,0:T(2,128)}, u32[]{:S(2)}) copy-start(f32[2,5]{1,0:T(2,128)} %get-tuple-element.5) | copy-start | bytes 124

commit v4 on v3

--- a/solution.py
+++ b/solution.py
@@ -11,6 +11,7 @@
 C = 32
 MESH = pl.DeviceIdType.MESH
 F32 = jnp.float32
+BF16 = jnp.bfloat16
 AXES = ("gx", "gy", "gz")
 DIRS = [
     (dx, dy, dz)
@@ -63,22 +64,40 @@
     return jnp.concatenate([field[:, t * 128 : t * 128 + 128] for t in range(8)], axis=0)
 
 
+def split(x):
+    high = x.astype(BF16)
+    rest = x - high.astype(F32)
+    middle = rest.astype(BF16)
+    return high, middle, (rest - middle.astype(F32)).astype(BF16)
+
+
+PAIRS = ((0, 0), (0, 1), (1, 0), (1, 1), (0, 2), (2, 0))
+
+
 def dot(left, right):
-    return lax.dot_general(
-        left,
-        right,
-        (((1,), (0,)), ((), ())),
-        precision=lax.Precision.HIGHEST,
-        preferred_element_type=F32,
-    )
+    return jnp.dot(left, right, preferred_element_type=F32)
+
+
+def spread(matrix):
+    parts = split(matrix)
+    return jnp.concatenate([parts[i] for i, _ in PAIRS], axis=1)
+
+
+def stack(field):
+    parts = split(field)
+    return jnp.concatenate([parts[i] for _, i in PAIRS], axis=0)
 
 
 def matvec(field, xmat_ref, ymat_ref, zmat_ref):
-    first = dot(xmat_ref[...], wide(field))
+    first = dot(xmat_ref[...], stack(wide(field)))
     mass, stiff = swap(tall(first[:C])), swap(tall(first[C:]))
-    second = dot(ymat_ref[...], jnp.concatenate([wide(stiff), wide(mass)], axis=0))
+    second = dot(ymat_ref[...], stack(jnp.concatenate([wide(stiff), wide(mass)], axis=0)))
     third = jnp.concatenate([tall(second[:C]), tall(second[C:])], axis=1)
-    return swap(dot(third, zmat_ref[...]))
+    high, middle, low = split(third)
+    pair = zmat_ref[:, 0:256]
+    both = dot(high, pair) + dot(middle, pair)
+    rest = dot(low, zmat_ref[:, 0:128]) + dot(high, zmat_ref[:, 256:384])
+    return swap(both[:, :128] + (both[:, 128:] + rest))
 
 
 def block_diagonal(matrix):
@@ -238,10 +257,12 @@
     for copy in inputs:
         copy.wait()
     kx, ky, kz, mx, my, mz = (stencils_ref[i] for i in range(6))
-    xmat[...] = jnp.concatenate([mx, kx], axis=0)
+    xmat[...] = spread(jnp.concatenate([mx, kx], axis=0))
     top = jnp.concatenate([my, ky], axis=1)
-    ymat[...] = jnp.concatenate([top, jnp.concatenate([jnp.zeros((C, C), F32), my], axis=1)], axis=0)
-    zmat[...] = jnp.concatenate([block_diagonal(mz.T), block_diagonal(kz.T)], axis=0)
+    ymat[...] = spread(jnp.concatenate([top, jnp.concatenate([jnp.zeros((C, C), F32), my], axis=1)], axis=0))
+    zmat[...] = jnp.concatenate(
+        split(jnp.concatenate([block_diagonal(mz.T), block_diagonal(kz.T)], axis=0)), axis=1
+    )
 
     def exchange_start(par):
         pack(out, sends.at[par])
@@ -445,9 +466,9 @@
             pltpu.VMEM((ITERS + 1, 256, 128), F32),
             pltpu.VMEM((ITERS, 256, 128), F32),
             pltpu.VMEM((256, 128), F32),
-            pltpu.VMEM((2 * C, C), F32),
-            pltpu.VMEM((2 * C, 2 * C), F32),
-            pltpu.VMEM((256, 128), F32),
+            pltpu.VMEM((2 * C, 6 * C), BF16),
+            pltpu.VMEM((2 * C, 12 * C), BF16),
+            pltpu.VMEM((256, 384), BF16),
             pltpu.VMEM((2, len(DIRS), 8, 128), F32),
             pltpu.VMEM((2, len(DIRS), 8, 128), F32),
             pltpu.VMEM((ITERS + 1, nx * ny * nz, 128), F32),

time: 51.3 us -> 48.3 us (0.942)
  Pallas kernels: 48 us -> 45 us
    pallas_call x1, Pallas kernels: 48 us -> 45 us  [shards(): pl.pallas_call(functools.partial(kernel, sizes), out_shape=(jax.ShapeDtyp...]
where the time goes in v4:
time: 48.3 us; the launch traced here: 48.2 us
  Pallas kernels  45 us (93%)
  local copies, waits for them, and re-layouts  2.55 us (5%)
  between operations  0.65 us (1%)
    pallas_call x1, Pallas kernels, shards(): pl.pallas_call(functools.partial(kernel, sizes), out_shape=(jax.ShapeDtyp...  45 us
    unnamed x4, local copies, waits for them, and re-layouts  2.55 us

profile of v4, /device:TPU:1, one launch (start us, length us, event | category | flops | bytes accessed | tf_op | source)
XLA Modules:
  0.0 48.2 jit_solution(152818156849560158)
XLA Ops:
  0.6 45.0 %shard_map.41 = (f32[5,32,1024]{2,1,0:T(8,128)}, f32[2,5]{1,0:T(2,128)}) custom-call(f32[32,1024]{1,0:T(8,128)} %bitcast.5, f32[6,32,32]{2,1,0:T(8,128)} %bitcast.6), custom_call_target="tpu_custom_call" | custom-call | tf_op jit(solution)/shard_map/pallas_call | solution.py:452
  45.6 0.0 copy-start
  45.7 2.0 %copy.6 = f32[1,1,1,1,5,32,1024]{6,5,4,3,2,1,0:T(8,128)} copy(f32[1,1,1,1,5,32,1024]{6,5,4,3,2,1,0:T(8,128)} %bitcast.4) | data formatting | bytes 1310720
  47.6 0.0 copy-done
  47.6 0.6 %copy.7 = f32[1,2,5]{2,1,0:T(2,128)} copy(f32[1,2,5]{2,1,0:T(2,128)S(1)} %bitcast.7) | data formatting | bytes 80
Async XLA Ops:
  45.6 2.0 %copy-start = (f32[2,5]{1,0:T(2,128)S(1)}, f32[2,5]{1,0:T(2,128)}, u32[]{:S(2)}) copy-start(f32[2,5]{1,0:T(2,128)} %get-tuple-element.5) | copy-start | bytes 124

commit v5 on v4

--- a/solution.py
+++ b/solution.py
@@ -1,4 +1,5 @@
 import functools
+import itertools
 
 import jax
 import jax.numpy as jnp
@@ -20,7 +21,9 @@
     for dz in (-1, 0, 1)
     if (dx, dy, dz) != (0, 0, 0)
 ]
-SLOT = {d: i for i, d in enumerate(DIRS)}
+TILES = [d for d in DIRS if d[0] == 0 or d[1:] == (0, 0)]
+ROWS = [d for d in DIRS if d not in TILES]
+SLOT = {d: i for dirs in (TILES, ROWS) for i, d in enumerate(dirs)}
 SHRINK = 2.0**-17
 
 
@@ -88,16 +91,16 @@
     return jnp.concatenate([parts[i] for _, i in PAIRS], axis=0)
 
 
-def matvec(field, xmat_ref, ymat_ref, zmat_ref):
-    first = dot(xmat_ref[...], stack(wide(field)))
+def matvec(field, first_ref, second_ref, zmat_ref):
+    first = dot(first_ref[...], stack(wide(field)))
     mass, stiff = swap(tall(first[:C])), swap(tall(first[C:]))
-    second = dot(ymat_ref[...], stack(jnp.concatenate([wide(stiff), wide(mass)], axis=0)))
+    second = dot(second_ref[...], stack(jnp.concatenate([wide(stiff), wide(mass)], axis=0)))
     third = jnp.concatenate([tall(second[:C]), tall(second[C:])], axis=1)
     high, middle, low = split(third)
     pair = zmat_ref[:, 0:256]
     both = dot(high, pair) + dot(middle, pair)
     rest = dot(low, zmat_ref[:, 0:128]) + dot(high, zmat_ref[:, 256:384])
-    return swap(both[:, :128] + (both[:, 128:] + rest))
+    return both[:, :128] + (both[:, 128:] + rest)
 
 
 def block_diagonal(matrix):
@@ -128,8 +131,9 @@
     return fine, tuple(at + d for at, d in zip(here, step))
 
 
-def pack(out_ref, send_ref):
+def pack(out_ref, tile_ref, row_ref):
     s, l = iota((8, 128), 0), iota((8, 128), 1)
+    line = iota((1, 128), 1)
     lower = lambda t, ai: out_ref[pl.ds(t * 32 + ai * 8, 8), :]
     zero = jnp.zeros((8, 128), F32)
     low, high = zero, zero
@@ -139,44 +143,52 @@
             moved = roll(lower(t, ai), r, 1)
             low = jnp.where(l % C == r, moved, low)
             high = jnp.where(l % C == (r + C - 1) % C, moved, high)
+
+    def send_row(d, plane, source, keep):
+        row_ref[pl.ds(SLOT[d], 1), :] = jnp.where(keep, plane[source : source + 1], 0.0)
+
+    for dx in (-1, 1):
+        source = 0 if dx < 0 else 7
+        for dz, plane, base in ((-1, low, 0), (1, high, -31)):
+            for dy in (-1, 0, 1):
+                keep = (line % C) // 8 == (3 if dx < 0 else 0)
+                if dy != 0:
+                    keep = keep & (line // C == (3 if dy < 0 else 0)) & (line % 8 == (7 if dy < 0 else 0))
+                send_row((dx, dy, dz), roll(plane, base - dx * 24 - dy * 103, 1), source, keep)
+        plane = out_ref[pl.ds(0 if dx < 0 else C - 1, 8, stride=C), :]
+        tile_ref[SLOT[(dx, 0, 0)]] = plane
+        for dy in (-1, 1):
+            keep = line // C == (3 if dy < 0 else 0)
+            send_row((dx, dy, 0), roll(plane, 96 if dy < 0 else 32, 1), 0 if dy < 0 else 7, keep)
     for dz, plane, base in ((-1, low, 0), (1, high, -31)):
-        for dx in (-1, 0, 1):
-            for dy in (-1, 0, 1):
-                lanes = base - dx * 24 - dy * 103
-                part = roll(roll(plane, lanes, 1), dx, 0)
-                keep = None
-                if dx != 0:
-                    keep = (s == (7 if dx < 0 else 0)) & ((l % C) // 8 == (3 if dx < 0 else 0))
-                if dy != 0:
-                    mine = (l // C == (3 if dy < 0 else 0)) & (l % 8 == (7 if dy < 0 else 0))
-                    keep = mine if keep is None else keep & mine
-                send_ref[SLOT[(dx, dy, dz)]] = part if keep is None else jnp.where(keep, part, 0.0)
-    for dx in (-1, 1):
-        plane = out_ref[pl.ds(0 if dx < 0 else C - 1, 8, stride=C), :]
-        send_ref[SLOT[(dx, 0, 0)]] = plane
+        tile_ref[SLOT[(0, 0, dz)]] = roll(plane, base, 1)
         for dy in (-1, 1):
-            part = roll(roll(plane, 96 if dy < 0 else 32, 1), dy, 0)
-            keep = (s == (7 if dy < 0 else 0)) & (l // C == (3 if dy < 0 else 0))
-            send_ref[SLOT[(dx, dy, 0)]] = jnp.where(keep, part, 0.0)
+            keep = (l // C == (3 if dy < 0 else 0)) & (l % 8 == (7 if dy < 0 else 0))
+            tile_ref[SLOT[(0, dy, dz)]] = jnp.where(keep, roll(plane, base - dy * 103, 1), 0.0)
     for dy in (-1, 1):
         plane = zero
         for ai in range(4):
             piece = roll(lower(0 if dy < 0 else 7, ai), C * (ai + (0 if dy < 0 else 1)), 1)
             plane = jnp.where(l // C == ai, piece, plane)
-        send_ref[SLOT[(0, dy, 0)]] = plane
-
-
-def unpack(out_ref, got_ref):
-    l = iota((8, 128), 1)
+        tile_ref[SLOT[(0, dy, 0)]] = plane
+
+
+def unpack(out_ref, tile_ref, row_ref):
+    s, l = iota((8, 128), 0), iota((8, 128), 1)
     near = (-1, 0, 1)
+    got = lambda *d: tile_ref[SLOT[d]]
+    row = lambda *d: row_ref[pl.ds(SLOT[d], 1), :]
+    ends = lambda last, first: jnp.where(s == 7, last, jnp.where(s == 0, first, 0.0))
     for dx in (-1, 1):
-        plane = sum(got_ref[SLOT[(dx, dy, 0)]] for dy in near)
+        plane = got(dx, 0, 0) + ends(row(dx, -1, 0), row(dx, 1, 0))
         rows = pl.ds(C - 1 if dx < 0 else 0, 8, stride=C)
         out_ref[rows, :] = out_ref[rows, :] + plane
     low, high = (
-        sum(got_ref[SLOT[(dx, dy, dz)]] for dx in near for dy in near) for dz in (1, -1)
+        sum(got(0, dy, dz) for dy in near)
+        + ends(sum(row(-1, dy, dz) for dy in near), sum(row(1, dy, dz) for dy in near))
+        for dz in (1, -1)
     )
-    first, last = got_ref[SLOT[(0, 1, 0)]], got_ref[SLOT[(0, -1, 0)]]
+    first, last = got(0, 1, 0), got(0, -1, 0)
     for t in range(8):
         for ai in range(4):
             r = ai * 8 + t
@@ -202,13 +214,16 @@
     small,
     out,
     powers,
+    turned,
     vecs,
     weights,
-    xmat,
-    ymat,
+    first,
+    second,
     zmat,
-    sends,
-    gots,
+    tiles,
+    rows,
+    got_tiles,
+    got_rows,
     terms,
     send_sem,
     got_sem,
@@ -228,19 +243,9 @@
     )
     along = [[lax.rem(at + k, size) for k in range(size)] for at, size in zip(here, sizes)]
     everyone = [tuple(along[a][d[a]] for a in range(3)) for d in steps if any(d)]
-    spans = [
-        1 + jnp.where(at > 0, 1, 0) + jnp.where(at < size - 1, 1, 0)
-        for at, size in zip(here, sizes)
+    beside = [
+        jnp.where(at > 0, 1, 0) + jnp.where(at < size - 1, 1, 0) for at, size in zip(here, sizes)
     ]
-    degree = spans[0] * spans[1] * spans[2] - 1
-    degrees = sorted(
-        {
-            i * j * k - 1
-            for i in span_set(nx)
-            for j in span_set(ny)
-            for k in span_set(nz)
-        }
-    )
 
     inputs = [
         pltpu.make_async_copy(start_hbm, start_ref, in_sem.at[0]),
@@ -248,7 +253,8 @@
     ]
     for copy in inputs:
         copy.start()
-    gots[...] = jnp.zeros_like(gots)
+    got_tiles[...] = jnp.zeros_like(got_tiles)
+    got_rows[...] = jnp.zeros_like(got_rows)
     barrier = pltpu.get_barrier_semaphore()
     for there in everyone:
         pl.semaphore_signal(barrier, inc=1, device_id=there, device_id_type=MESH)
@@ -257,47 +263,57 @@
     for copy in inputs:
         copy.wait()
     kx, ky, kz, mx, my, mz = (stencils_ref[i] for i in range(6))
-    xmat[...] = spread(jnp.concatenate([mx, kx], axis=0))
-    top = jnp.concatenate([my, ky], axis=1)
-    ymat[...] = spread(jnp.concatenate([top, jnp.concatenate([jnp.zeros((C, C), F32), my], axis=1)], axis=0))
+    empty = jnp.zeros((C, C), F32)
+    for i, (mass, stiff) in enumerate(((mx, kx), (my, ky))):
+        first[i] = spread(jnp.concatenate([mass, stiff], axis=0))
+        upper, lower = (jnp.concatenate(p, axis=1) for p in ((mass, stiff), (empty, mass)))
+        second[1 - i] = spread(jnp.concatenate([upper, lower], axis=0))
     zmat[...] = jnp.concatenate(
         split(jnp.concatenate([block_diagonal(mz.T), block_diagonal(kz.T)], axis=0)), axis=1
     )
 
     def exchange_start(par):
-        pack(out, sends.at[par])
-        if True:
-            for d in sorted(DIRS, key=lambda d: -sum(abs(i) for i in d)):
-                fine, there = neighbour(sizes, here, d)
-
-                @pl.when(fine)
-                def _():
-                    pltpu.make_async_remote_copy(
-                        src_ref=sends.at[par, SLOT[d]],
-                        dst_ref=gots.at[par, SLOT[d]],
-                        send_sem=send_sem.at[par],
-                        recv_sem=got_sem.at[par],
-                        device_id=there,
-                        device_id_type=MESH,
-                    ).start()
+        pack(out, tiles.at[par], rows.at[par])
+        for d in sorted(DIRS, key=lambda d: -sum(abs(i) for i in d)):
+            fine, there = neighbour(sizes, here, (d[1], d[0], d[2]) if par else d)
+            if d in TILES:
+                source, target = tiles.at[par, SLOT[d]], got_tiles.at[par, SLOT[d]]
+            else:
+                source, target = rows.at[par, pl.ds(SLOT[d], 1)], got_rows.at[par, pl.ds(SLOT[d], 1)]
+
+            @pl.when(fine)
+            def _():
+                pltpu.make_async_remote_copy(
+                    src_ref=source,
+                    dst_ref=target,
+                    send_sem=send_sem.at[par, int(d in ROWS)],
+                    recv_sem=got_sem.at[par, int(d in ROWS)],
+                    device_id=there,
+                    device_id_type=MESH,
+                ).start()
 
     def exchange_end(par):
-        for n in degrees:
-
-            @pl.when(degree == n)
+        order = (1, 0, 2) if par else (0, 1, 2)
+        counts = message_counts(*(beside[i] for i in order))
+        choices = [{0} if n == 1 else {1} if n == 2 else {1, 2} for n in (sizes[i] for i in order)]
+        for n, m in sorted({message_counts(*c) for c in itertools.product(*choices)}):
+
+            @pl.when((counts[0] == n) & (counts[1] == m))
             def _():
-                both = pltpu.make_async_remote_copy(
-                    src_ref=sends.at[par, pl.ds(0, n)],
-                    dst_ref=gots.at[par, pl.ds(0, n)],
-                    send_sem=send_sem.at[par],
-                    recv_sem=got_sem.at[par],
-                    device_id=everyone[0],
-                    device_id_type=MESH,
-                )
-                both.wait_recv()
-                both.wait_send()
-
-        unpack(out, gots.at[par])
+                for kind, (count, sent, got) in enumerate(((n, tiles, got_tiles), (m, rows, got_rows))):
+                    if count:
+                        both = pltpu.make_async_remote_copy(
+                            src_ref=sent.at[par, pl.ds(0, count)],
+                            dst_ref=got.at[par, pl.ds(0, count)],
+                            send_sem=send_sem.at[par, kind],
+                            recv_sem=got_sem.at[par, kind],
+                            device_id=everyone[0],
+                            device_id_type=MESH,
+                        )
+                        both.wait_recv()
+                        both.wait_send()
+
+        unpack(out, got_tiles.at[par], got_rows.at[par])
 
     def gather_start(k, pairs):
         s, l = iota((8, 128), 0), iota((8, 128), 1)
@@ -374,13 +390,23 @@
     exchange_end(0)
     powers[0] = out[...]
 
-    out[...] = matvec(powers[0], xmat, ymat, zmat)
-    exchange_start(1)
+    def apply(j):
+        here = (turned if j % 2 else powers)[j]
+        out[...] = matvec(here, first.at[j % 2], second.at[j % 2], zmat)
+        exchange_start((j + 1) % 2)
+
+    def turn(j):
+        if j % 2:
+            powers[j] = swap(turned[j])
+        else:
+            turned[j] = swap(powers[j])
+
+    apply(0)
     exchange_end(1)
-    powers[1] = out[...]
-
-    out[...] = matvec(powers[1], xmat, ymat, zmat)
-    exchange_start(0)
+    turned[1] = out[...]
+
+    apply(1)
+    turn(1)
     weighted = weights[...] * powers[1]
     gather_start(1, [(powers[0], weights[...] * powers[0]), (powers[0], weighted), (powers[1], weighted)])
     (size,) = gather_end(0, 1)
@@ -390,8 +416,8 @@
     triangle, alphas, betas = [], [], []
     for j in range(2, ITERS + 1):
         if j < ITERS:
-            out[...] = matvec(powers[j], xmat, ymat, zmat)
-            exchange_start((j + 1) % 2)
+            apply(j)
+            turn(j)
         weighted = weights[...] * powers[j]
         earlier = [vecs[k] if j > 2 else powers[0] for k in range(j - 1)]
         gather_start(j, [(v, weighted) for v in earlier + [powers[j - 1], powers[j]]])
@@ -417,7 +443,8 @@
             betas.append(triangle[k][k] * hess[(k, i)] / triangle[i][i])
         if j < ITERS:
             exchange_end((j + 1) % 2)
-            new = out[...] - alphas[j - 2] * powers[j]
+            side = powers if j % 2 else turned
+            new = out[...] - alphas[j - 2] * side[j]
             lead = betas[j - 2]
             if j == 2:
                 lead = lead * triangle[0][0]
@@ -425,8 +452,12 @@
                 behind = betas[j - 3]
                 if j == 3:
                     behind = behind / triangle[0][0]
-                new = new - behind * powers[j - 1]
-            powers[j + 1] = new * (1.0 / lead)
+                new = new - behind * side[j - 1]
+            new = new * (1.0 / lead)
+            if j + 1 == ITERS:
+                powers[ITERS] = swap(new) if j % 2 == 0 else new
+            else:
+                side[j + 1] = new
             hess[(j, j)], hess[(j + 1, j)] = alphas[j - 2], lead
 
     s, l = iota((8, 128), 0), iota((8, 128), 1)
@@ -441,8 +472,8 @@
     last.wait()
 
 
-def span_set(size):
-    return {1} if size == 1 else {2} if size == 2 else {2, 3}
+def message_counts(x, y, z):
+    return x + y + z + y * z, x * (y + z + y * z)
 
 
 def shards(sizes, start, stencils):
@@ -465,15 +496,18 @@
             pltpu.VMEM((256, 128), F32),
             pltpu.VMEM((ITERS + 1, 256, 128), F32),
             pltpu.VMEM((ITERS, 256, 128), F32),
+            pltpu.VMEM((ITERS, 256, 128), F32),
             pltpu.VMEM((256, 128), F32),
-            pltpu.VMEM((2 * C, 6 * C), BF16),
-            pltpu.VMEM((2 * C, 12 * C), BF16),
+            pltpu.VMEM((2, 2 * C, 6 * C), BF16),
+            pltpu.VMEM((2, 2 * C, 12 * C), BF16),
             pltpu.VMEM((256, 384), BF16),
-            pltpu.VMEM((2, len(DIRS), 8, 128), F32),
-            pltpu.VMEM((2, len(DIRS), 8, 128), F32),
+            pltpu.VMEM((2, len(TILES), 8, 128), F32),
+            pltpu.VMEM((2, len(ROWS), 128), F32),
+            pltpu.VMEM((2, len(TILES), 8, 128), F32),
+            pltpu.VMEM((2, len(ROWS), 128), F32),
             pltpu.VMEM((ITERS + 1, nx * ny * nz, 128), F32),
         ]
-        + [pltpu.SemaphoreType.DMA((2,))] * 2
+        + [pltpu.SemaphoreType.DMA((2, 2))] * 2
         + [pltpu.SemaphoreType.DMA((ITERS + 1,))] * 2
         + [pltpu.SemaphoreType.DMA((2,)), pltpu.SemaphoreType.DMA((ITERS + 1,))],
         compiler_params=pltpu.CompilerParams(collective_id=0, has_side_effects=True),

time: 48.3 us -> 45.6 us (0.944)
  Pallas kernels: 45 us -> 42.3 us
    pallas_call x1, Pallas kernels: 45 us -> 42.3 us  [shards(): pl.pallas_call(functools.partial(kernel, sizes), out_shape=(jax.ShapeDtyp...]
where the time goes in v5:
time: 45.6 us; the launch traced here: 45.5 us
  Pallas kernels  42.3 us (93%)
  local copies, waits for them, and re-layouts  2.55 us (6%)
  between operations  0.65 us (1%)
    pallas_call x1, Pallas kernels, shards(): pl.pallas_call(functools.partial(kernel, sizes), out_shape=(jax.ShapeDtyp...  42.3 us
    unnamed x4, local copies, waits for them, and re-layouts  2.55 us

profile of v5, /device:TPU:1, one launch (start us, length us, event | category | flops | bytes accessed | tf_op | source)
XLA Modules:
  0.0 45.5 jit_solution(4377903238085309569)
XLA Ops:
  0.6 42.3 %shard_map.41 = (f32[5,32,1024]{2,1,0:T(8,128)}, f32[2,5]{1,0:T(2,128)}) custom-call(f32[32,1024]{1,0:T(8,128)} %bitcast.5, f32[6,32,32]{2,1,0:T(8,128)} %bitcast.6), custom_call_target="tpu_custom_call" | custom-call | tf_op jit(solution)/shard_map/pallas_call | solution.py:483
  42.9 0.0 copy-start
  42.9 2.0 %copy.6 = f32[1,1,1,1,5,32,1024]{6,5,4,3,2,1,0:T(8,128)} copy(f32[1,1,1,1,5,32,1024]{6,5,4,3,2,1,0:T(8,128)} %bitcast.4) | data formatting | bytes 1310720
  44.9 0.0 copy-done
  44.9 0.6 %copy.7 = f32[1,2,5]{2,1,0:T(2,128)} copy(f32[1,2,5]{2,1,0:T(2,128)S(1)} %bitcast.7) | data formatting | bytes 80
Async XLA Ops:
  42.9 2.0 %copy-start = (f32[2,5]{1,0:T(2,128)S(1)}, f32[2,5]{1,0:T(2,128)}, u32[]{:S(2)}) copy-start(f32[2,5]{1,0:T(2,128)} %get-tuple-element.5) | copy-start | bytes 124

commit v6 on v5

--- a/solution.py
+++ b/solution.py
@@ -216,6 +216,8 @@
     powers,
     turned,
     vecs,
+    turned_vecs,
+    turned_weights,
     weights,
     first,
     second,
@@ -225,10 +227,13 @@
     got_tiles,
     got_rows,
     terms,
+    marks,
     send_sem,
     got_sem,
     term_send,
     term_got,
+    mark_send,
+    mark_got,
     in_sem,
     out_sem,
 ):
@@ -256,8 +261,21 @@
     got_tiles[...] = jnp.zeros_like(got_tiles)
     got_rows[...] = jnp.zeros_like(got_rows)
     barrier = pltpu.get_barrier_semaphore()
-    for there in everyone:
+    line = [(gx, gy, lax.rem(gz + k, nz)) for k in range(1, nz)]
+    plane = [
+        (along[0][i], along[1][k], gz) for i in range(nx) for k in range(ny) if (i, k) != (0, 0)
+    ]
+    for there in plane + line:
         pl.semaphore_signal(barrier, inc=1, device_id=there, device_id_type=MESH)
+    for d in DIRS:
+        if d[2] != 0 and d[:2] != (0, 0):
+            fine, there = neighbour(sizes, here, d)
+
+            @pl.when(fine)
+            def _():
+                pl.semaphore_signal(barrier, inc=1, device_id=there, device_id_type=MESH)
+
+    greetings = len(plane) + len(line) + beside[2] * ((1 + beside[0]) * (1 + beside[1]) - 1)
 
     weights[...] = weight_field(sizes, here)
     for copy in inputs:
@@ -336,6 +354,32 @@
                 device_id=there,
                 device_id_type=MESH,
             ).start()
+
+    def mark_start(k, at, peers, row):
+        marks[k, pl.ds(at, 1)] = row
+        for there in peers:
+            pltpu.make_async_remote_copy(
+                src_ref=marks.at[k, pl.ds(at, 1)],
+                dst_ref=marks.at[k, pl.ds(at, 1)],
+                send_sem=mark_send.at[k],
+                recv_sem=mark_got.at[k],
+                device_id=there,
+                device_id_type=MESH,
+            ).start()
+
+    def mark_end(k, peers):
+        if peers:
+            both = pltpu.make_async_remote_copy(
+                src_ref=marks.at[k, pl.ds(0, len(peers))],
+                dst_ref=marks.at[k, pl.ds(0, len(peers))],
+                send_sem=mark_send.at[k],
+                recv_sem=mark_got.at[k],
+                device_id=peers[0],
+                device_id_type=MESH,
+            )
+            both.wait_recv()
+            both.wait_send()
+        return jnp.sum(marks[k, 0 : len(peers) + 1], axis=0, keepdims=True)
 
     def gather_end(k, count):
         others = pl.ds(0, len(everyone))
@@ -364,6 +408,8 @@
         new = new * (1.0 / height[i])
         if i < ITERS:
             vecs[i] = new
+        if i < ITERS - 1:
+            turned_vecs[i] = swap(new)
         if i > 0:
             wides[i - 1] = wide(new)
             leaving(i).start()
@@ -382,13 +428,14 @@
         return found
 
     out[...] = tall(start_ref[...]) * weights[...] * SHRINK
-    pl.semaphore_wait(barrier, len(everyone))
+    pl.semaphore_wait(barrier, greetings)
     exchange_start(0)
     trace = [jnp.sum(jnp.where(iota((C, C), 0) == iota((C, C), 1), m, 0.0), keepdims=True) / C for m in (kx, ky, kz, mx, my, mz)]
     mean = trace[0] * trace[4] * trace[5] + trace[3] * trace[1] * trace[5] + trace[3] * trace[4] * trace[2]
-    gather_row(0, jnp.broadcast_to(mean / (nx * ny * nz), (1, 128)))
+    mark_start(0, gz, line, jnp.broadcast_to(mean / (nx * ny * nz), (1, 128)))
     exchange_end(0)
     powers[0] = out[...]
+    mark_start(1, gx * ny + gy, plane, mark_end(0, line))
 
     def apply(j):
         here = (turned if j % 2 else powers)[j]
@@ -407,9 +454,10 @@
 
     apply(1)
     turn(1)
+    turned_weights[...] = swap(weights[...])
+    size = mark_end(1, plane)
     weighted = weights[...] * powers[1]
     gather_start(1, [(powers[0], weights[...] * powers[0]), (powers[0], weighted), (powers[1], weighted)])
-    (size,) = gather_end(0, 1)
     exchange_end(0)
     powers[2] = out[...] * (1.0 / size)
 
@@ -418,9 +466,19 @@
         if j < ITERS:
             apply(j)
             turn(j)
-        weighted = weights[...] * powers[j]
-        earlier = [vecs[k] if j > 2 else powers[0] for k in range(j - 1)]
-        gather_start(j, [(v, weighted) for v in earlier + [powers[j - 1], powers[j]]])
+        if j < ITERS:
+            weighted = weights[...] * powers[j]
+            earlier = [vecs[k] if j > 2 else powers[0] for k in range(j - 1)] + [powers[j - 1]]
+            image = powers[j]
+        else:
+            weighted = turned_weights[...] * turned[j]
+            earlier = [turned_vecs[k] for k in range(j - 1)] + [turned[j - 1]]
+            image = turned[j]
+        if j == 2:
+            earlier = [powers[0], powers[1]]
+        gather_start(j, [(v, weighted) for v in earlier + [image]])
+        if j == ITERS:
+            powers[j] = swap(image)
         rounds = [j - 1] if j < ITERS else [j - 1, j]
         for k in rounds:
             if k == 1:
@@ -454,10 +512,7 @@
                     behind = behind / triangle[0][0]
                 new = new - behind * side[j - 1]
             new = new * (1.0 / lead)
-            if j + 1 == ITERS:
-                powers[ITERS] = swap(new) if j % 2 == 0 else new
-            else:
-                side[j + 1] = new
+            side[j + 1] = new
             hess[(j, j)], hess[(j + 1, j)] = alphas[j - 2], lead
 
     s, l = iota((8, 128), 0), iota((8, 128), 1)
@@ -474,6 +529,20 @@
 
 def message_counts(x, y, z):
     return x + y + z + y * z, x * (y + z + y * z)
+
+
+def hand_over(basis_in, coefficients_in, basis_out, coefficients_out, wides, small, in_sem, out_sem):
+    pairs = [(basis_in.at[i], wides.at[i], basis_out.at[i]) for i in range(ITERS)]
+    pairs.append((coefficients_in, small, coefficients_out))
+    come = [pltpu.make_async_copy(a, b, in_sem.at[i]) for i, (a, b, _) in enumerate(pairs)]
+    go = [pltpu.make_async_copy(b, c, out_sem.at[i]) for i, (_, b, c) in enumerate(pairs)]
+    for copy in come:
+        copy.start()
+    for first, then in zip(come, go):
+        first.wait()
+        then.start()
+    for copy in go:
+        copy.wait()
 
 
 def shards(sizes, start, stencils):
@@ -495,8 +564,10 @@
             pltpu.VMEM((2, ITERS), F32),
             pltpu.VMEM((256, 128), F32),
             pltpu.VMEM((ITERS + 1, 256, 128), F32),
+            pltpu.VMEM((ITERS + 1, 256, 128), F32),
             pltpu.VMEM((ITERS, 256, 128), F32),
-            pltpu.VMEM((ITERS, 256, 128), F32),
+            pltpu.VMEM((ITERS - 1, 256, 128), F32),
+            pltpu.VMEM((256, 128), F32),
             pltpu.VMEM((256, 128), F32),
             pltpu.VMEM((2, 2 * C, 6 * C), BF16),
             pltpu.VMEM((2, 2 * C, 12 * C), BF16),
@@ -506,12 +577,29 @@
             pltpu.VMEM((2, len(TILES), 8, 128), F32),
             pltpu.VMEM((2, len(ROWS), 128), F32),
             pltpu.VMEM((ITERS + 1, nx * ny * nz, 128), F32),
+            pltpu.VMEM((2, max(nx * ny, nz), 128), F32),
         ]
         + [pltpu.SemaphoreType.DMA((2, 2))] * 2
         + [pltpu.SemaphoreType.DMA((ITERS + 1,))] * 2
+        + [pltpu.SemaphoreType.DMA((2,))] * 2
         + [pltpu.SemaphoreType.DMA((2,)), pltpu.SemaphoreType.DMA((ITERS + 1,))],
         compiler_params=pltpu.CompilerParams(collective_id=0, has_side_effects=True),
     )(start.reshape(C, C * C), stencils.reshape(6, C, C))
+    basis, coefficients = pl.pallas_call(
+        hand_over,
+        out_shape=(
+            jax.ShapeDtypeStruct((ITERS, C, C * C), F32),
+            jax.ShapeDtypeStruct((2, ITERS), F32),
+        ),
+        in_specs=[anyw, anyw],
+        out_specs=(anyw, anyw),
+        scratch_shapes=[
+            pltpu.VMEM((ITERS, C, C * C), F32),
+            pltpu.VMEM((2, ITERS), F32),
+            pltpu.SemaphoreType.DMA((ITERS + 1,)),
+            pltpu.SemaphoreType.DMA((ITERS + 1,)),
+        ],
+    )(basis, coefficients)
     return (
         basis.reshape(1, 1, 1, 1, ITERS, C, C * C),
         coefficients.reshape(1, 2, ITERS),

time: 45.6 us -> 44.1 us (0.967)
  local copies, waits for them, and re-layouts: 2.55 us -> 0 us
  Pallas kernels: 42.3 us -> 43.3 us
    unnamed x4 -> x0, local copies, waits for them, and re-layouts: 2.55 us -> none
    pallas_call x0 -> x1, Pallas kernels: none -> 1.93 us  [shards(): pl.pallas_call(hand_over, out_shape=(jax.ShapeDtypeStruct((ITERS, C, C *...]
    pallas_call x1, Pallas kernels: 42.3 us -> 41.3 us  [shards(): pl.pallas_call(functools.partial(kernel, sizes), out_shape=(jax.ShapeDtyp...]
where the time goes in v6:
time: 44.1 us; the launch traced here: 43.9 us
  Pallas kernels  43.3 us (98%)
  between operations  0.64 us (1%)
    pallas_call x1, Pallas kernels, shards(): pl.pallas_call(functools.partial(kernel, sizes), out_shape=(jax.ShapeDtyp...  41.3 us
    pallas_call x1, Pallas kernels, shards(): pl.pallas_call(hand_over, out_shape=(jax.ShapeDtypeStruct((ITERS, C, C *...  1.93 us

profile of v6, /device:TPU:1, one launch (start us, length us, event | category | flops | bytes accessed | tf_op | source)
XLA Modules:
  0.0 43.9 jit_solution(8480273267737474621)
XLA Ops:
  0.6 41.3 %shard_map.41 = (f32[5,32,1024]{2,1,0:T(8,128)}, f32[2,5]{1,0:T(2,128)}) custom-call(f32[32,1024]{1,0:T(8,128)} %bitcast.4, f32[6,32,32]{2,1,0:T(8,128)} %bitcast.5), custom_call_target="tpu_custom_call" | custom-call | tf_op jit(solution)/shard_map/pallas_call | solution.py:552
  42.0 1.9 %shard_map.42 = (f32[5,32,1024]{2,1,0:T(8,128)}, f32[2,5]{1,0:T(2,128)}) custom-call(f32[5,32,1024]{2,1,0:T(8,128)} %get-tuple-element.6.basis_in, f32[2,5]{1,0:T(2,128)} %get-tuple-element.7.coefficients_in), custom_call_target="tpu_custom_call" | custom-call | tf_op jit(solution)/shard_map/pallas_call | solution.py:588

commit v7 on v6

--- a/solution.py
+++ b/solution.py
@@ -218,6 +218,10 @@
     vecs,
     turned_vecs,
     turned_weights,
+    lifted,
+    turned_lifted,
+    images,
+    shifting,
     weights,
     first,
     second,
@@ -462,58 +466,74 @@
     powers[2] = out[...] * (1.0 / size)
 
     triangle, alphas, betas = [], [], []
+    shifts = {2: size}
     for j in range(2, ITERS + 1):
         if j < ITERS:
             apply(j)
             turn(j)
-        if j < ITERS:
-            weighted = weights[...] * powers[j]
-            earlier = [vecs[k] if j > 2 else powers[0] for k in range(j - 1)] + [powers[j - 1]]
-            image = powers[j]
+            if j == 2:
+                lifted[j] = powers[2] - 2.0 * powers[1] + size * powers[0]
+            else:
+                lifted[j] = powers[j] + shifting[...]
+            weighted = weights[...] * lifted[j]
+            earlier = [powers[0], powers[1]] if j == 2 else [vecs[k] for k in range(j - 1)] + [lifted[j - 1]]
+            image = lifted[j]
         else:
-            weighted = turned_weights[...] * turned[j]
-            earlier = [turned_vecs[k] for k in range(j - 1)] + [turned[j - 1]]
             image = turned[j]
-        if j == 2:
-            earlier = [powers[0], powers[1]]
+            weighted = turned_weights[...] * image
+            earlier = [turned_vecs[k] for k in range(j - 1)] + [turned_lifted[...]]
         gather_start(j, [(v, weighted) for v in earlier + [image]])
         if j == ITERS:
-            powers[j] = swap(image)
-        rounds = [j - 1] if j < ITERS else [j - 1, j]
-        for k in rounds:
+            lifted[j] = swap(image)
+        for k in [j - 1] if j < ITERS else [j - 1, j]:
             if k == 1:
                 square, *rest = gather_end(1, 3)
                 triangle.append([jnp.sqrt(square)])
+                start_size = triangle[0][0]
                 settle(0, powers[0], triangle[0])
                 triangle.append(heights(rest, triangle))
-                hess = {(1, 0): 1.0, (1, 1): 0.0, (2, 1): size}
+                settle(1, powers[1], triangle[1])
+                alphas.append(triangle[1][0] / start_size)
+                betas.append(triangle[1][1] / start_size)
+                images[0] = powers[1] * (1.0 / (start_size * size))
             else:
                 products = gather_end(k, k + 1)
+                scale = size
                 if k == 2:
-                    products[0] = products[0] / triangle[0][0]
+                    products[0] = products[0] / start_size
+                    scale = size / start_size
                 triangle.append(heights(products, triangle))
-            settle(k, powers[k], triangle[k])
-            i = k - 1
-            diagonal = triangle[k][i] * hess[(k, i)] / triangle[i][i]
-            if i > 0:
-                diagonal = diagonal + hess[(i, i)] - triangle[i][i - 1] * hess[(i, i - 1)] / triangle[i - 1][i - 1]
-            alphas.append(diagonal)
-            betas.append(triangle[k][k] * hess[(k, i)] / triangle[i][i])
-        if j < ITERS:
-            exchange_end((j + 1) % 2)
-            side = powers if j % 2 else turned
-            new = out[...] - alphas[j - 2] * side[j]
-            lead = betas[j - 2]
-            if j == 2:
-                lead = lead * triangle[0][0]
-            else:
-                behind = betas[j - 3]
-                if j == 3:
-                    behind = behind / triangle[0][0]
-                new = new - behind * side[j - 1]
-            new = new * (1.0 / lead)
-            side[j + 1] = new
-            hess[(j, j)], hess[(j + 1, j)] = alphas[j - 2], lead
+                settle(k, lifted[k], triangle[k])
+                scale = scale / betas[k - 2]
+                alphas.append(2.0 * shifts[k] - alphas[k - 2] + triangle[k][k - 1] * scale)
+                betas.append(triangle[k][k] * scale)
+        if j == ITERS:
+            break
+        image = powers[j] * (1.0 / start_size) if j == 2 else powers[j] - betas[j - 3] * images[j - 3]
+        image = (image - alphas[j - 2] * images[j - 2]) * (1.0 / betas[j - 2])
+        images[j - 1] = image
+        shift = shifts[j + 1] = alphas[j - 2]
+        change = (shift * shift / size) * vecs[j - 1] - (2.0 * shift) * image
+        if j + 1 < ITERS:
+            shifting[...] = change
+        else:
+            shifting[...] = swap(change)
+            turned_lifted[...] = swap(lifted[j])
+        exchange_end((j + 1) % 2)
+        side = powers if j % 2 else turned
+        new = out[...] - alphas[j - 2] * side[j]
+        lead = betas[j - 2]
+        if j == 2:
+            lead = lead * start_size
+        else:
+            behind = betas[j - 3]
+            if j == 3:
+                behind = behind / start_size
+            new = new - behind * side[j - 1]
+        new = new * (1.0 / lead)
+        if j + 1 == ITERS:
+            new = new + shifting[...]
+        side[j + 1] = new
 
     s, l = iota((8, 128), 0), iota((8, 128), 1)
     tile = jnp.zeros((8, 128), F32)
@@ -566,6 +586,10 @@
             pltpu.VMEM((ITERS + 1, 256, 128), F32),
             pltpu.VMEM((ITERS + 1, 256, 128), F32),
             pltpu.VMEM((ITERS, 256, 128), F32),
+            pltpu.VMEM((ITERS - 1, 256, 128), F32),
+            pltpu.VMEM((256, 128), F32),
+            pltpu.VMEM((ITERS + 1, 256, 128), F32),
+            pltpu.VMEM((256, 128), F32),
             pltpu.VMEM((ITERS - 1, 256, 128), F32),
             pltpu.VMEM((256, 128), F32),
             pltpu.VMEM((256, 128), F32),

time: 44.1 us -> 44.1 us (level)
  no operation moved by 1% of the time
where the time goes in v7:
time: 44.1 us; the launch traced here: 43.9 us
  Pallas kernels  43.3 us (98%)
  between operations  0.64 us (1%)
    pallas_call x1, Pallas kernels, shards(): pl.pallas_call(functools.partial(kernel, sizes), out_shape=(jax.ShapeDtyp...  41.3 us
    pallas_call x1, Pallas kernels, shards(): pl.pallas_call(hand_over, out_shape=(jax.ShapeDtypeStruct((ITERS, C, C *...  1.93 us

profile of v7, /device:TPU:1, one launch (start us, length us, event | category | flops | bytes accessed | tf_op | source)
XLA Modules:
  0.0 43.9 jit_solution(7048974590120180089)
XLA Ops:
  0.6 41.3 %shard_map.41 = (f32[5,32,1024]{2,1,0:T(8,128)}, f32[2,5]{1,0:T(2,128)}) custom-call(f32[32,1024]{1,0:T(8,128)} %bitcast.4, f32[6,32,32]{2,1,0:T(8,128)} %bitcast.5), custom_call_target="tpu_custom_call" | custom-call | tf_op jit(solution)/shard_map/pallas_call | solution.py:572
  42.0 1.9 %shard_map.42 = (f32[5,32,1024]{2,1,0:T(8,128)}, f32[2,5]{1,0:T(2,128)}) custom-call(f32[5,32,1024]{2,1,0:T(8,128)} %get-tuple-element.6.basis_in, f32[2,5]{1,0:T(2,128)} %get-tuple-element.7.coefficients_in), custom_call_target="tpu_custom_call" | custom-call | tf_op jit(solution)/shard_map/pallas_call | solution.py:612

commit v8 on v7

--- a/solution.py
+++ b/solution.py
@@ -296,7 +296,7 @@
 
     def exchange_start(par):
         pack(out, tiles.at[par], rows.at[par])
-        for d in sorted(DIRS, key=lambda d: -sum(abs(i) for i in d)):
+        for d in sorted(DIRS, key=lambda d: -(2 * abs(d[0]) + 2 * abs(d[1]) + abs(d[2]))):
             fine, there = neighbour(sizes, here, (d[1], d[0], d[2]) if par else d)
             if d in TILES:
                 source, target = tiles.at[par, SLOT[d]], got_tiles.at[par, SLOT[d]]
@@ -409,7 +409,7 @@
         new = image
         for k in range(i):
             new = new - height[k] * vecs[k]
-        new = new * (1.0 / height[i])
+        new = new * height[i + 1]
         if i < ITERS:
             vecs[i] = new
         if i < ITERS - 1:
@@ -425,10 +425,11 @@
         last = with_last
         for k in range(i - 1):
             last = last - known[i - 1][k] * found[k]
-        found.append(last / known[i - 1][i - 1])
+        found.append(last * known[i - 1][i])
         for value in found:
             square = square - value * value
-        found.append(jnp.sqrt(square))
+        over = lax.rsqrt(square)
+        found += [square * over, over]
         return found
 
     out[...] = tall(start_ref[...]) * weights[...] * SHRINK
@@ -458,19 +459,21 @@
 
     apply(1)
     turn(1)
-    turned_weights[...] = swap(weights[...])
     size = mark_end(1, plane)
+    over_size = 1.0 / size
     weighted = weights[...] * powers[1]
     gather_start(1, [(powers[0], weights[...] * powers[0]), (powers[0], weighted), (powers[1], weighted)])
+    turned_weights[...] = swap(weights[...])
     exchange_end(0)
-    powers[2] = out[...] * (1.0 / size)
-
-    triangle, alphas, betas = [], [], []
+    powers[2] = out[...] * over_size
+
+    triangle, alphas, betas, over_betas = [], [], [], []
     shifts = {2: size}
     for j in range(2, ITERS + 1):
         if j < ITERS:
             apply(j)
-            turn(j)
+            if j % 2:
+                turn(j)
             if j == 2:
                 lifted[j] = powers[2] - 2.0 * powers[1] + size * powers[0]
             else:
@@ -485,35 +488,39 @@
         gather_start(j, [(v, weighted) for v in earlier + [image]])
         if j == ITERS:
             lifted[j] = swap(image)
+        elif j % 2 == 0:
+            turn(j)
         for k in [j - 1] if j < ITERS else [j - 1, j]:
             if k == 1:
                 square, *rest = gather_end(1, 3)
-                triangle.append([jnp.sqrt(square)])
-                start_size = triangle[0][0]
+                triangle.append([jnp.sqrt(square), lax.rsqrt(square)])
+                start_size, over_start = triangle[0]
                 settle(0, powers[0], triangle[0])
                 triangle.append(heights(rest, triangle))
                 settle(1, powers[1], triangle[1])
-                alphas.append(triangle[1][0] / start_size)
-                betas.append(triangle[1][1] / start_size)
-                images[0] = powers[1] * (1.0 / (start_size * size))
+                alphas.append(triangle[1][0] * over_start)
+                betas.append(triangle[1][1] * over_start)
+                over_betas.append(triangle[1][2] * start_size)
+                images[0] = powers[1] * (over_start * over_size)
             else:
                 products = gather_end(k, k + 1)
-                scale = size
+                scale, over_scale = size, over_size
                 if k == 2:
-                    products[0] = products[0] / start_size
-                    scale = size / start_size
+                    products[0] = products[0] * over_start
+                    scale, over_scale = size * over_start, over_size * start_size
                 triangle.append(heights(products, triangle))
                 settle(k, lifted[k], triangle[k])
-                scale = scale / betas[k - 2]
+                scale = scale * over_betas[k - 2]
                 alphas.append(2.0 * shifts[k] - alphas[k - 2] + triangle[k][k - 1] * scale)
                 betas.append(triangle[k][k] * scale)
+                over_betas.append(triangle[k][k + 1] * (over_scale * betas[k - 2]))
         if j == ITERS:
             break
-        image = powers[j] * (1.0 / start_size) if j == 2 else powers[j] - betas[j - 3] * images[j - 3]
-        image = (image - alphas[j - 2] * images[j - 2]) * (1.0 / betas[j - 2])
+        image = powers[j] * over_start if j == 2 else powers[j] - betas[j - 3] * images[j - 3]
+        image = (image - alphas[j - 2] * images[j - 2]) * over_betas[j - 2]
         images[j - 1] = image
         shift = shifts[j + 1] = alphas[j - 2]
-        change = (shift * shift / size) * vecs[j - 1] - (2.0 * shift) * image
+        change = (shift * shift * over_size) * vecs[j - 1] - (2.0 * shift) * image
         if j + 1 < ITERS:
             shifting[...] = change
         else:
@@ -522,15 +529,15 @@
         exchange_end((j + 1) % 2)
         side = powers if j % 2 else turned
         new = out[...] - alphas[j - 2] * side[j]
-        lead = betas[j - 2]
+        over_lead = over_betas[j - 2]
         if j == 2:
-            lead = lead * start_size
+            over_lead = over_lead * over_start
         else:
             behind = betas[j - 3]
             if j == 3:
-                behind = behind / start_size
+                behind = behind * over_start
             new = new - behind * side[j - 1]
-        new = new * (1.0 / lead)
+        new = new * over_lead
         if j + 1 == ITERS:
             new = new + shifting[...]
         side[j + 1] = new

time: 44.1 us -> 43.7 us (level)
  no operation moved by 1% of the time
where the time goes in v8:
time: 43.7 us; the launch traced here: 43.6 us
  Pallas kernels  42.9 us (98%)
  between operations  0.64 us (1%)
    pallas_call x1, Pallas kernels, shards(): pl.pallas_call(functools.partial(kernel, sizes), out_shape=(jax.ShapeDtyp...  41 us
    pallas_call x1, Pallas kernels, shards(): pl.pallas_call(hand_over, out_shape=(jax.ShapeDtypeStruct((ITERS, C, C *...  1.93 us

profile of v8, /device:TPU:1, one launch (start us, length us, event | category | flops | bytes accessed | tf_op | source)
XLA Modules:
  0.0 43.6 jit_solution(10792991283152913002)
XLA Ops:
  0.6 41.0 %shard_map.41 = (f32[5,32,1024]{2,1,0:T(8,128)}, f32[2,5]{1,0:T(2,128)}) custom-call(f32[32,1024]{1,0:T(8,128)} %bitcast.4, f32[6,32,32]{2,1,0:T(8,128)} %bitcast.5), custom_call_target="tpu_custom_call" | custom-call | tf_op jit(solution)/shard_map/pallas_call | solution.py:579
  41.6 1.9 %shard_map.42 = (f32[5,32,1024]{2,1,0:T(8,128)}, f32[2,5]{1,0:T(2,128)}) custom-call(f32[5,32,1024]{2,1,0:T(8,128)} %get-tuple-element.6.basis_in, f32[2,5]{1,0:T(2,128)} %get-tuple-element.7.coefficients_in), custom_call_target="tpu_custom_call" | custom-call | tf_op jit(solution)/shard_map/pallas_call | solution.py:619

commit v9 on v8

--- a/solution.py
+++ b/solution.py
@@ -128,7 +128,7 @@
         if d != 0:
             inside = at > 0 if d < 0 else at < size - 1
             fine = inside if fine is None else jnp.logical_and(fine, inside)
-    return fine, tuple(at + d for at, d in zip(here, step))
+    return fine, tuple(lax.rem(at + d + size, size) if d else at for size, at, d in zip(sizes, here, step))
 
 
 def pack(out_ref, tile_ref, row_ref):

time: 43.7 us -> 43.7 us (level)
  no operation moved by 1% of the time
where the time goes in v9:
time: 43.7 us; the launch traced here: 43.6 us
  Pallas kernels  42.9 us (98%)
  between operations  0.64 us (1%)
    pallas_call x1, Pallas kernels, shards(): pl.pallas_call(functools.partial(kernel, sizes), out_shape=(jax.ShapeDtyp...  41 us
    pallas_call x1, Pallas kernels, shards(): pl.pallas_call(hand_over, out_shape=(jax.ShapeDtypeStruct((ITERS, C, C *...  1.93 us

profile of v9, /device:TPU:1, one launch (start us, length us, event | category | flops | bytes accessed | tf_op | source)
XLA Modules:
  0.0 43.6 jit_solution(1676463592147578748)
XLA Ops:
  0.6 41.0 %shard_map.41 = (f32[5,32,1024]{2,1,0:T(8,128)}, f32[2,5]{1,0:T(2,128)}) custom-call(f32[32,1024]{1,0:T(8,128)} %bitcast.4, f32[6,32,32]{2,1,0:T(8,128)} %bitcast.5), custom_call_target="tpu_custom_call" | custom-call | tf_op jit(solution)/shard_map/pallas_call | solution.py:579
  41.6 1.9 %shard_map.42 = (f32[5,32,1024]{2,1,0:T(8,128)}, f32[2,5]{1,0:T(2,128)}) custom-call(f32[5,32,1024]{2,1,0:T(8,128)} %get-tuple-element.6.basis_in, f32[2,5]{1,0:T(2,128)} %get-tuple-element.7.coefficients_in), custom_call_target="tpu_custom_call" | custom-call | tf_op jit(solution)/shard_map/pallas_call | solution.py:619

commit v10 on v8

--- a/solution.py
+++ b/solution.py
@@ -412,7 +412,7 @@
         new = new * height[i + 1]
         if i < ITERS:
             vecs[i] = new
-        if i < ITERS - 1:
+        if i == ITERS - 2:
             turned_vecs[i] = swap(new)
         if i > 0:
             wides[i - 1] = wide(new)
@@ -490,6 +490,12 @@
             lifted[j] = swap(image)
         elif j % 2 == 0:
             turn(j)
+        if j == ITERS - 2:
+            turned_vecs[0] = swap(vecs[0])
+            turned_vecs[1] = swap(vecs[1])
+        if j == ITERS - 1:
+            turned_vecs[2] = swap(vecs[2])
+            turned_lifted[...] = swap(lifted[j])
         for k in [j - 1] if j < ITERS else [j - 1, j]:
             if k == 1:
                 square, *rest = gather_end(1, 3)
@@ -525,7 +531,6 @@
             shifting[...] = change
         else:
             shifting[...] = swap(change)
-            turned_lifted[...] = swap(lifted[j])
         exchange_end((j + 1) % 2)
         side = powers if j % 2 else turned
         new = out[...] - alphas[j - 2] * side[j]

time: 43.7 us -> 43.7 us (level)
  no operation moved by 1% of the time
where the time goes in v10:
time: 43.7 us; the launch traced here: 43.5 us
  Pallas kernels  42.9 us (98%)
  between operations  0.64 us (1%)
    pallas_call x1, Pallas kernels, shards(): pl.pallas_call(functools.partial(kernel, sizes), out_shape=(jax.ShapeDtyp...  40.9 us
    pallas_call x1, Pallas kernels, shards(): pl.pallas_call(hand_over, out_shape=(jax.ShapeDtypeStruct((ITERS, C, C *...  1.93 us

profile of v10, /device:TPU:1, one launch (start us, length us, event | category | flops | bytes accessed | tf_op | source)
XLA Modules:
  0.0 43.5 jit_solution(16209046465904037314)
XLA Ops:
  0.6 40.9 %shard_map.41 = (f32[5,32,1024]{2,1,0:T(8,128)}, f32[2,5]{1,0:T(2,128)}) custom-call(f32[32,1024]{1,0:T(8,128)} %bitcast.4, f32[6,32,32]{2,1,0:T(8,128)} %bitcast.5), custom_call_target="tpu_custom_call" | custom-call | tf_op jit(solution)/shard_map/pallas_call | solution.py:584
  41.6 1.9 %shard_map.42 = (f32[5,32,1024]{2,1,0:T(8,128)}, f32[2,5]{1,0:T(2,128)}) custom-call(f32[5,32,1024]{2,1,0:T(8,128)} %get-tuple-element.6.basis_in, f32[2,5]{1,0:T(2,128)} %get-tuple-element.7.coefficients_in), custom_call_target="tpu_custom_call" | custom-call | tf_op jit(solution)/shard_map/pallas_call | solution.py:624
